TPU v7x, 32 devices: a whole 2x2x4 slice. The times are simulated.
32 devices in a mesh: tp: 4 (over z), fsdp: 8 (over y, x, core).
Axes of the slice: x: 2, y: 2, z: 4, core: 2. Of those that a mesh axis runs over, the one named last changes fastest.
Arguments:
- x_in: bfloat16 [24, 768, 2048], P('fsdp')
- dy_out: bfloat16 [24, 768, 2048], P('fsdp')
- ln_gain: float32 [2048], P('fsdp')
- w_q: bfloat16 [2048, 2048], P('fsdp', 'tp')
- w_k: bfloat16 [2048, 256], P('fsdp')
- w_v: bfloat16 [2048, 256], P('fsdp')
- w_o: bfloat16 [2048, 2048], P('tp', 'fsdp')
- w_gate: bfloat16 [2048, 8192], P('fsdp', 'tp')
- w_up: bfloat16 [2048, 8192], P('fsdp', 'tp')
- w_down: bfloat16 [8192, 2048], P('tp', 'fsdp')
Outputs:
- output 1: bfloat16 [24, 768, 2048], P('fsdp')
- output 2: bfloat16 [24, 768, 2048], P('fsdp')
- output 3: float32 [2048], P('fsdp')
- output 4: float32 [2048, 2048], P('fsdp', 'tp')
- output 5: float32 [2048, 256], P('fsdp')
- output 6: float32 [2048, 256], P('fsdp')
- output 7: float32 [2048, 2048], P('tp', 'fsdp')
- output 8: float32 [2048, 8192], P('fsdp', 'tp')
- output 9: float32 [2048, 8192], P('fsdp', 'tp')
- output 10: float32 [8192, 2048], P('tp', 'fsdp')
All inputs are finite; a program needn't handle non-finite values.
Results may differ from a plain program's by a relative error of at most 0.0152999.
Values are sent between devices in bfloat16 or wider.
A program may use at most 1 GiB of HBM per device.

v0:
```python
import math
import jax
import jax.numpy as jnp
from jax import lax
from jax.sharding import PartitionSpec as P


def layer_norm(x_f32, gain):
    x_mean = jnp.mean(x_f32, axis=-1, keepdims=True)
    x_cent = x_f32 - x_mean
    x_var = jnp.mean(x_cent * x_cent, axis=-1, keepdims=True)
    return (x_cent * lax.rsqrt(x_var + 1e-5) * gain).astype(jnp.bfloat16)


def rotate(vals, cos_t, sin_t):
    half_dim = vals.shape[-1] // 2
    first = vals[..., :half_dim]
    second = vals[..., half_dim:]
    return jnp.concatenate([first * cos_t - second * sin_t, second * cos_t + first * sin_t], axis=-1)


def qk_post(q_raw, k_raw):
    seq_len = k_raw.shape[1]
    head_dim = k_raw.shape[2]
    half_dim = head_dim // 2
    inv_freq = jnp.power(10000.0, -2.0 * jnp.arange(half_dim, dtype=jnp.float32) / head_dim)
    angle = jnp.arange(seq_len, dtype=jnp.float32)[:, None] * inv_freq[None, :]
    cos_t = jnp.cos(angle)
    sin_t = jnp.sin(angle)
    q_rot = rotate(q_raw.astype(jnp.float32), cos_t[:, None, :], sin_t[:, None, :]) * (1.0 / math.sqrt(head_dim))
    k_rot = rotate(k_raw.astype(jnp.float32), cos_t, sin_t)
    return q_rot.astype(jnp.bfloat16), k_rot.astype(jnp.bfloat16)


def attend(q_rot, k_rot, v_val):
    seq_len = q_rot.shape[1]
    causal = lax.broadcasted_iota(jnp.int32, (seq_len, 1, seq_len), 0) >= lax.broadcasted_iota(jnp.int32, (seq_len, 1, seq_len), 2)
    scores = jnp.einsum('crie,cle->cril', q_rot, k_rot, preferred_element_type=jnp.float32)
    scores = jnp.where(causal, scores, -1e30)
    row_max = lax.stop_gradient(jnp.max(scores, axis=-1, keepdims=True))
    exp_val = jnp.exp(scores - row_max)
    att_prob = (exp_val / jnp.sum(exp_val, axis=-1, keepdims=True)).astype(jnp.bfloat16)
    return jnp.einsum('cril,cle->crie', att_prob, v_val, preferred_element_type=jnp.float32).astype(jnp.bfloat16)


def swiglu(gate_val, up_val):
    return (jax.nn.silu(gate_val.astype(jnp.float32)) * up_val.astype(jnp.float32)).astype(jnp.bfloat16)


def matmul_f32(form, left, right):
    return jnp.einsum(form, left, right, preferred_element_type=jnp.float32)


def gather_rows(w_part):
    return lax.all_gather(w_part, 'fsdp', axis=0, tiled=True)


def gather_cols(w_part):
    return lax.all_gather(w_part, 'fsdp', axis=1, tiled=True)


def scatter_rows(grad_full):
    return lax.psum_scatter(grad_full, 'fsdp', scatter_dimension=0, tiled=True)


def scatter_cols(grad_full):
    return lax.psum_scatter(grad_full, 'fsdp', scatter_dimension=1, tiled=True)


def solution(mesh):
    def device_step(x_in, dy_out, ln_gain, w_q, w_k, w_v, w_o, w_gate, w_up, w_down):
        n_batch, seq_len, _ = x_in.shape
        head_dim = w_k.shape[1]
        gain_full = lax.all_gather(ln_gain, 'fsdp', tiled=True)
        x_f32 = x_in.astype(jnp.float32)
        h_norm, norm_pull = jax.vjp(layer_norm, x_f32, gain_full)
        wq_full = gather_rows(w_q)
        wk_full = gather_rows(w_k)
        wv_full = gather_rows(w_v)
        wg_full = gather_rows(w_gate)
        wu_full = gather_rows(w_up)
        q_raw = matmul_f32('bsd,de->bse', h_norm, wq_full).astype(jnp.bfloat16)
        k_raw = matmul_f32('bsd,de->bse', h_norm, wk_full).astype(jnp.bfloat16)
        v_val = matmul_f32('bsd,de->bse', h_norm, wv_full).astype(jnp.bfloat16)
        gate_val = matmul_f32('bsd,df->bsf', h_norm, wg_full).astype(jnp.bfloat16)
        up_val = matmul_f32('bsd,df->bsf', h_norm, wu_full).astype(jnp.bfloat16)
        q_heads = q_raw.reshape(n_batch, seq_len, -1, head_dim)
        (q_rot, k_rot), rope_pull = jax.vjp(qk_post, q_heads, k_raw)
        att_out, att_pull = jax.vjp(attend, q_rot, k_rot, v_val)
        mlp_act, act_pull = jax.vjp(swiglu, gate_val, up_val)
        att_flat = att_out.reshape(n_batch, seq_len, -1)
        wo_full = gather_cols(w_o)
        wd_full = gather_cols(w_down)
        branch_part = (matmul_f32('bse,ed->bsd', att_flat, wo_full) + matmul_f32('bsf,fd->bsd', mlp_act, wd_full)).astype(jnp.bfloat16)
        branch_sum = lax.psum(branch_part, 'tp')
        y_out = (x_f32 + branch_sum.astype(jnp.float32)).astype(jnp.bfloat16)

        wo_back = gather_cols(w_o)
        wd_back = gather_cols(w_down)
        grad_wo = scatter_cols(matmul_f32('bse,bsd->ed', att_flat, dy_out))
        grad_wdown = scatter_cols(matmul_f32('bsf,bsd->fd', mlp_act, dy_out))
        d_att = matmul_f32('bsd,ed->bse', dy_out, wo_back).astype(jnp.bfloat16).reshape(n_batch, seq_len, -1, head_dim)
        d_act = matmul_f32('bsd,fd->bsf', dy_out, wd_back).astype(jnp.bfloat16)
        d_gate, d_up = act_pull(d_act)
        d_qrot, dk_part, dv_part = att_pull(d_att)
        kv_sum = lax.psum(jnp.concatenate([dk_part, dv_part], axis=-1).astype(jnp.float32), 'tp')
        d_krot = kv_sum[..., :head_dim].astype(jnp.bfloat16)
        d_val = kv_sum[..., head_dim:].astype(jnp.bfloat16)
        d_qraw, d_kraw = rope_pull((d_qrot, d_krot))
        d_qflat = d_qraw.reshape(n_batch, seq_len, -1)
        grad_wq = scatter_rows(matmul_f32('bsd,bse->de', h_norm, d_qflat))
        grad_wk = scatter_rows(matmul_f32('bsd,bse->de', h_norm, d_kraw))
        grad_wv = scatter_rows(matmul_f32('bsd,bse->de', h_norm, d_val))
        grad_wgate = scatter_rows(matmul_f32('bsd,bsf->df', h_norm, d_gate))
        grad_wup = scatter_rows(matmul_f32('bsd,bsf->df', h_norm, d_up))
        wq_back = gather_rows(w_q)
        wk_back = gather_rows(w_k)
        wv_back = gather_rows(w_v)
        wg_back = gather_rows(w_gate)
        wu_back = gather_rows(w_up)
        dh_part = (matmul_f32('bse,de->bsd', d_qflat, wq_back) + matmul_f32('bsf,df->bsd', d_gate, wg_back) + matmul_f32('bsf,df->bsd', d_up, wu_back)).astype(jnp.bfloat16)
        dh_sum = lax.psum(dh_part, 'tp')
        dh_full = (dh_sum.astype(jnp.float32) + matmul_f32('bse,de->bsd', d_kraw, wk_back) + matmul_f32('bse,de->bsd', d_val, wv_back)).astype(jnp.bfloat16)
        dx_norm, gain_part = norm_pull(dh_full)
        grad_x = (dy_out.astype(jnp.float32) + dx_norm).astype(jnp.bfloat16)
        grad_gain = lax.psum_scatter(gain_part, 'fsdp', scatter_dimension=0, tiled=True)
        return (y_out, grad_x, grad_gain, grad_wq, grad_wk, grad_wv, grad_wo, grad_wgate, grad_wup, grad_wdown)

    act_spec = P('fsdp', None, None)
    row_spec = P('fsdp', 'tp')
    kv_spec = P('fsdp', None)
    col_spec = P('tp', 'fsdp')
    in_specs = (act_spec, act_spec, P('fsdp'), row_spec, kv_spec, kv_spec, col_spec, row_spec, row_spec, col_spec)
    out_specs = (act_spec, act_spec, P('fsdp'), row_spec, kv_spec, kv_spec, col_spec, row_spec, row_spec, col_spec)
    return jax.shard_map(device_step, mesh=mesh, in_specs=in_specs, out_specs=out_specs, check_vma=False)
```

profile of v0, /device:TPU:0, one launch (start us, length us, event | category | flops | bytes accessed | tf_op | source)
XLA Modules:
  0.0 1756.6 jit_solution(14020041744731364595)
XLA Ops:
  15.1 11.0 all-gather
  26.1 5.0 convert_reduce_fusion
  31.2 2.6 fusion.11
  36.5 6.9 fusion.71
  44.8 16.7 all-gather.13.cloned.1.call-done
  61.5 6.8 fusion.72
  68.3 23.5 %all-gather.9.cloned.1.call-done = bf16[2048,512]{0,1:T(8,128)(2,1)} async-done(((bf16[256,512]{0,1:T(8,128)(2,1)}), bf16[2048,512]{0,1:T(8,128)(2,1)}) %all-gather.9.cloned.1.call-update) | async-done | bytes 2097168 | tf_op jit(solution)/shard_map/all_gather | solution.py:55
  91.8 9.5 fusion.65
  101.3 2.6 fusion.115
  106.0 3.2 copy.144
  109.3 4.3 multiply_subtract_fusion
  113.6 12.5 fusion.116
  126.2 9.4 fusion.68
  135.6 9.6 fusion.24
  145.4 11.0 convert_multiply_fusion.8
  159.8 5.5 convolution_convert_fusion.1
  165.3 9.2 fusion.61
  174.6 9.1 fusion.59
  183.7 26.3 %fusion.53 = bf16[3,768,2048]{2,1,0:T(8,128)(2,1)} fusion(bf16[3,768,2048]{2,1,0:T(8,128)(2,1)} %param.11, bf16[2048,2048]{1,0:T(8,128)(2,1)} %all-gather.21.cloned.1.call-done), kind=kOutput, calls=%fused_computation.69 | convolution fusion | flops 19332071424 | bytes 27262976 | tf_op jit(solution)/shard_map/bsd,fd->bsf/dot_general | solution.py:51
  210.0 24.3 %all-gather.19.cloned.1.call-done = bf16[2048,2048]{1,0:T(8,128)(2,1)} async-done(((bf16[256,2048]{1,0:T(8,128)(2,1)}), bf16[2048,2048]{1,0:T(8,128)(2,1)}) %all-gather.19.cloned.1.call-update) | async-done | bytes 8388624 | tf_op jit(solution)/shard_map/all_gather | solution.py:55
  234.3 26.1 %fusion.50 = bf16[3,768,2048]{2,1,0:T(8,128)(2,1)} fusion(bf16[2048,2048]{1,0:T(8,128)(2,1)} %all-gather.19.cloned.1.call-done, bf16[3,768,2048]{2,1,0:T(8,128)(2,1)} %param.10, f32[2048]{0:T(1024)S(1)} %bitcast.130, f32[3,768]{1,0:T(4,128)S(1)} %fusion.85, f32[3,768]{1,0:T(4,128)S(1)} %broadcast_multiply_fusion), kind=kOutput, calls=%fused_computation.68 | convolution fusion | flops 19355664384 | bytes 27289600 | tf_op jit(solution)/shard_map/bsd,df->bsf/dot_general | solution.py:51
  260.4 29.7 %all-gather.17.cloned.1.call-done = bf16[2048,2048]{1,0:T(8,128)(2,1)} async-done(((bf16[256,2048]{1,0:T(8,128)(2,1)}), bf16[2048,2048]{1,0:T(8,128)(2,1)}) %all-gather.17.cloned.1.call-update) | async-done | bytes 8388624 | tf_op jit(solution)/shard_map/all_gather | solution.py:55
  290.1 34.9 %fusion.19 = (bf16[3,768,2048]{2,1,0:T(8,128)(2,1)}, bf16[3,768,2048]{2,1,0:T(8,128)(2,1)}) fusion(bf16[3,768,2048]{2,1,0:T(8,128)(2,1)} %fusion.50, bf16[3,768,2048]{2,1,0:T(8,128)(2,1)} %fusion.53, bf16[2048,2048]{1,0:T(8,128)(2,1)} %all-gather.17.cloned.1.call-done, bf16[3,768,2048]{2,1,0:T(8,128)(2,1)} %param.10, f32[2048]{0:T(1024)S(1)} %bitcast.131, ...), kind=kOutput, calls=%fused_computation.32 | convolution fusion | flops 19421724672 | bytes 55601152 | tf_op jit(solution)/shard_map/bsd,df->bsf/dot_general | solution.py:51
  325.0 28.9 %fusion.33 = f32[3,768,2048]{2,1,0:T(8,128)} fusion(bf16[2048,2048]{1,0:T(8,128)(2,1)} %all-gather.19.cloned.1.call-done, bf16[3,768,2048]{2,1,0:T(8,128)(2,1)} %fusion.53, bf16[3,768,2048]{2,1,0:T(8,128)(2,1)} %get-tuple-element.34), kind=kOutput, calls=%fused_computation.56 | convolution fusion | flops 19365101568 | bytes 46137344 | tf_op jit(solution)/shard_map/bsf,df->bsd/dot_general | solution.py:51
  354.0 30.5 %add_convert_fusion.3 = bf16[3,768,2048]{2,1,0:T(8,128)(2,1)} fusion(f32[3,768,2048]{2,1,0:T(8,128)} %fusion.59, bf16[2048,2048]{1,0:T(8,128)(2,1)} %all-gather.21.cloned.1.call-done, bf16[3,768,2048]{2,1,0:T(8,128)(2,1)} %fusion.50, bf16[3,768,2048]{2,1,0:T(8,128)(2,1)} %get-tuple-element.34), kind=kOutput, calls=%fused_computation.36 | convolution fusion | flops 19374538752 | bytes 55574528 | tf_op jit(solution)/shard_map/bsf,fd->bsd/dot_general | solution.py:51
  384.5 30.8 %add_convert_fusion.2 = bf16[3,768,2048]{2,1,0:T(8,128)(2,1)} fusion(f32[3,768,2048]{2,1,0:T(8,128)} %fusion.33, f32[3,768,2048]{2,1,0:T(8,128)} %fusion.61, bf16[3,768,2048]{2,1,0:T(8,128)(2,1)} %get-tuple-element.33, bf16[2048,2048]{1,0:T(8,128)(2,1)} %all-gather.17.cloned.1.call-done), kind=kOutput, calls=%fused_computation.35 | convolution fusion | flops 19341508608 | bytes 65011712 | tf_op jit(solution)/shard_map/bsf,df->bsd/dot_general | solution.py:51
  415.4 5.9 bitcast_convert_fusion
  421.3 9.1 bitcast_convert_fusion.1
  433.0 316.1 %all-reduce.10 = bf16[3,768,512]{1,2,0:T(8,128)(2,1)S(1)} all-reduce(f32[3,768,512]{1,2,0:T(8,128)} %maximum_convert_fusion), channel_id=1, replica_groups=mesh['tp'=4,'fsdp'=8] {'tp'}, use_global_device_ids=true, to_apply=%region_7.8 | all-reduce | flops 1179648 | bytes 7077888 | tf_op jit(solution)/shard_map/psum | solution.py:106
  749.2 10.3 convolution_bitcast_fusion.5
  761.5 9.5 convolution_bitcast_fusion.6
  771.1 9.9 convolution_bitcast_fusion.3
  781.5 11.5 convolution_bitcast_fusion.4
  793.0 28.5 %convolution_bitcast_fusion = f32[2048,2048]{1,0:T(8,128)} fusion(bf16[3,768,2048]{2,1,0:T(8,128)(2,1)} %param.11, bf16[3,768,2048]{2,1,0:T(8,128)(2,1)} %fusion.50, bf16[3,768,2048]{2,1,0:T(8,128)(2,1)} %get-tuple-element.34), kind=kOutput, calls=%fused_computation.49 | convolution fusion | flops 19365101568 | bytes 45088768 | tf_op jit(solution)/shard_map/bsf,bsd->fd/dot_general | solution.py:51
  821.8 33.9 %convolution_bitcast_fusion.1 = f32[2048,2048]{1,0:T(8,128)} fusion(bf16[3,768,2048]{2,1,0:T(8,128)(2,1)} %fusion.53, bf16[3,768,2048]{2,1,0:T(8,128)(2,1)} %get-tuple-element.34, bf16[3,768,2048]{2,1,0:T(8,128)(2,1)} %param.10, f32[2048]{0:T(1024)S(1)} %bitcast.136, f32[3,768]{1,0:T(4,128)S(1)} %copy-done.26, f32[3,768]{1,0:T(4,128)S(1)} %copy-done.15), kind=kOutput, calls=%fused_computation.50 | convolution fusion | flops 19388694528 | bytes 45115392 | tf_op jit(solution)/shard_map/bsd,bsf->df/dot_general | solution.py:51
  856.0 29.9 %convolution_bitcast_fusion.2 = f32[2048,2048]{1,0:T(8,128)} fusion(bf16[3,768,2048]{2,1,0:T(8,128)(2,1)} %get-tuple-element.33, bf16[3,768,2048]{2,1,0:T(8,128)(2,1)} %param.10, f32[2048]{0:T(1024)S(1)} %bitcast.137, f32[3,768]{1,0:T(4,128)S(1)} %copy-done.26, f32[3,768]{1,0:T(4,128)S(1)} %copy-done.15), kind=kOutput, calls=%fused_computation.51 | convolution fusion | flops 19350945792 | bytes 35678208 | tf_op jit(solution)/shard_map/bsd,bsf->df/dot_general | solution.py:51
  887.8 10.9 fusion.77
  898.6 295.1 %all-reduce.9.cloned.1.call-done = (bf16[3,768,2048]{2,1,0:T(8,128)(2,1)}, bf16[3,768,2048]{2,1,0:T(8,128)(2,1)}) async-done(((bf16[3,768,2048]{2,1,0:T(8,128)(2,1)}, bf16[3,768,2048]{2,1,0:T(8,128)(2,1)}), (bf16[3,768,2048]{2,1,0:T(8,128)(2,1)}, bf16[3,768,2048]{2,1,0:T(8,128)(2,1)})) %all-reduce.9.cloned.1.call-update) | async-done | bytes 18874384 | tf_op jit(solution)/shard_map/psum | solution.py:95
  1193.8 21.5 %fusion.12 = (f32[3,768]{1,0:T(4,128)S(1)}, bf16[3,768,2048]{2,1,0:T(8,128)(2,1)}) fusion(bf16[3,768,2048]{2,1,0:T(8,128)(2,1)} %param.10, f32[2048]{0:T(1024)} %bitcast.132, f32[3,768]{1,0:T(4,128)S(1)} %copy-done.15, bf16[2048,256]{1,0:T(8,128)(2,1)} %all-gather.13.cloned.1.call-done, bf16[3,768,512]{1,2,0:T(8,128)(2,1)S(1)} %copy-done.2, ...), kind=kOutput, calls=%fused_computation.25 | convolution fusion | flops 2463102720 | bytes 49443840 | tf_op jit(solution)/shard_map/bse,de->bsd/dot_general | solution.py:51
  1215.3 12.5 fusion.10
  1227.8 13.8 all-reduce.4
  1242.3 21.7 %add_convert_fusion = (bf16[3,768,2048]{2,1,0:T(8,128)(2,1)}, bf16[3,768,2048]{2,1,0:T(8,128)(2,1)}) fusion(bf16[3,768,2048]{2,1,0:T(8,128)(2,1)} %param.11, bf16[3,768,2048]{2,1,0:T(8,128)(2,1)} %param.10, bf16[3,768,2048]{2,1,0:T(8,128)(2,1)} %get-tuple-element.36, f32[3,768]{1,0:T(4,128)S(1)} %negate_multiply_fusion, ...), kind=kLoop, calls=%fused_computation.33 | loop fusion | flops 70778880 | bytes 56668160 | tf_op jit(solution)/shard_map/convert_element_type | solution.py:125
  1263.9 18.4 %reduce-scatter.10.cloned.1.call-done = f32[256,256]{1,0:T(8,128)} async-done(((f32[2048,256]{1,0:T(8,128)}), f32[256,256]{1,0:T(8,128)}) %reduce-scatter.10.cloned.1.call-update) | async-done | bytes 262160 | tf_op jit(solution)/shard_map/reduce_scatter | solution.py:63
  1282.4 54.8 %reduce-scatter.14.cloned.1.call-done = f32[512,256]{1,0:T(8,128)} async-done(((f32[512,2048]{1,0:T(8,128)}), f32[512,256]{1,0:T(8,128)}) %reduce-scatter.14.cloned.1.call-update) | async-done | bytes 524304 | tf_op jit(solution)/shard_map/reduce_scatter | solution.py:67
  1337.1 54.6 %reduce-scatter.8.cloned.1.call-done = f32[256,512]{1,0:T(8,128)} async-done(((f32[2048,512]{1,0:T(8,128)}), f32[256,512]{1,0:T(8,128)}) %reduce-scatter.8.cloned.1.call-update) | async-done | bytes 524304 | tf_op jit(solution)/shard_map/reduce_scatter | solution.py:63
  1391.7 119.4 %reduce-scatter.20.cloned.1.call-done = f32[2048,256]{1,0:T(8,128)} async-done(((f32[2048,2048]{1,0:T(8,128)}), f32[2048,256]{1,0:T(8,128)}) %reduce-scatter.20.cloned.1.call-update) | async-done | bytes 2097168 | tf_op jit(solution)/shard_map/reduce_scatter | solution.py:67
  1511.2 119.3 %reduce-scatter.18.cloned.1.call-done = f32[256,2048]{1,0:T(8,128)} async-done(((f32[2048,2048]{1,0:T(8,128)}), f32[256,2048]{1,0:T(8,128)}) %reduce-scatter.18.cloned.1.call-update) | async-done | bytes 2097168 | tf_op jit(solution)/shard_map/reduce_scatter | solution.py:63
  1630.5 119.3 %reduce-scatter.16.cloned.1.call-done = f32[256,2048]{1,0:T(8,128)} async-done(((f32[2048,2048]{1,0:T(8,128)}), f32[256,2048]{1,0:T(8,128)}) %reduce-scatter.16.cloned.1.call-update) | async-done | bytes 2097168 | tf_op jit(solution)/shard_map/reduce_scatter | solution.py:63
  (135 shorter events, 25.0 us)
Async XLA Ops:
  7.2 29.3 %all-gather.11.cloned.1.call-start = ((), (), s32[]{:S(2)}) async-start(), calls=%async_computation.8 | async-start | bytes 1179648 | tf_op jit(solution)/shard_map/all_gather | solution.py:55
  8.9 52.6 %all-gather.13.cloned.1.call-start = ((), (), s32[]{:S(2)}) async-start(), calls=%async_computation.9 | async-start | bytes 1179648 | tf_op jit(solution)/shard_map/all_gather | solution.py:55
  9.7 82.1 %all-gather.9.cloned.1.call-start = ((), (), s32[]{:S(2)}) async-start(), calls=%async_computation.7 | async-start | bytes 2359296 | tf_op jit(solution)/shard_map/all_gather | solution.py:55
  11.5 114.6 %all-gather.15.cloned.1.call-start = ((), (), s32[]{:S(2)}) async-start(), calls=%async_computation.10 | async-start | bytes 2359296 | tf_op jit(solution)/shard_map/all_gather | solution.py:59
  12.1 171.6 %all-gather.21.cloned.1.call-start = ((), (), s32[]{:S(2)}) async-start(), calls=%async_computation.13 | async-start | bytes 9437184 | tf_op jit(solution)/shard_map/all_gather | solution.py:59
  12.7 221.6 %all-gather.19.cloned.1.call-start = ((), (), s32[]{:S(2)}) async-start(), calls=%async_computation.12 | async-start | bytes 9437184 | tf_op jit(solution)/shard_map/all_gather | solution.py:55
  13.3 276.9 %all-gather.17.cloned.1.call-start = ((), (), s32[]{:S(2)}) async-start(), calls=%async_computation.11 | async-start | bytes 9437184 | tf_op jit(solution)/shard_map/all_gather | solution.py:55
  14.0 1179.7 %all-reduce.9.cloned.1.call-start = ((), (), s32[]{:S(2)}) async-start(), calls=%async_computation.21 | async-start | bytes 37748736 | tf_op jit(solution)/shard_map/psum | solution.py:95
  14.1 17.1 copy-start
  26.1 264.0 %copy-start.20 = (f32[8,1,256]{2,1,0:T(1,128)}, f32[8,1,256]{2,1,0:T(1,128)S(1)}, u32[]{:S(2)}) copy-start(f32[8,1,256]{2,1,0:T(1,128)S(1)} %all-gather) | copy-start | bytes 24580
  31.2 259.0 %copy-start.14 = (f32[3,768]{1,0:T(4,128)}, f32[3,768]{1,0:T(4,128)S(1)}, u32[]{:S(2)}) copy-start(f32[3,768]{1,0:T(4,128)S(1)} %broadcast_multiply_fusion) | copy-start | bytes 27652
  33.8 256.3 %copy-start.25 = (f32[3,768]{1,0:T(4,128)}, f32[3,768]{1,0:T(4,128)S(1)}, u32[]{:S(2)}) copy-start(f32[3,768]{1,0:T(4,128)S(1)} %fusion.85) | copy-start | bytes 27652
  35.3 8.1 copy-start.3
  35.3 8.1 copy-start.5
  126.1 19.3 %copy-start.28 = (f32[3,768,2]{1,2,0:T(2,128)}, f32[3,768,2]{1,2,0:T(2,128)S(1)}, u32[]{:S(2)}) copy-start(f32[3,768,2]{1,2,0:T(2,128)S(1)} %get-tuple-element.30) | copy-start | bytes 55300
  126.1 9.5 copy-start.37
  135.6 9.7 copy-start.35
  135.6 9.7 copy-start.16
  135.6 9.7 copy-start.18
  135.6 9.7 copy-start.19
  145.3 11.1 copy-start.38
  145.3 11.1 copy-start.30
  159.8 5.5 copy-start.32
  165.3 9.2 copy-start.34
  165.3 9.2 copy-start.33
  415.3 6.0 copy-start.10
  415.3 6.0 copy-start.17
  415.3 6.0 copy-start.29
  415.3 6.0 copy-start.31
  415.3 848.6 %reduce-scatter.12.cloned.1.call-start = ((), (), s32[]{:S(2)}) async-start(), calls=%async_computation.16 | async-start | bytes 2359296 | tf_op jit(solution)/shard_map/reduce_scatter | solution.py:63
  415.4 5.9 copy-start.11
  430.4 318.7 %copy-start.15 = (f32[3,768]{1,0:T(4,128)S(1)}, f32[3,768]{1,0:T(4,128)}, u32[]{:S(2)}) copy-start(f32[3,768]{1,0:T(4,128)} %copy-done.14) | copy-start | bytes 27652
  430.4 318.7 %copy-start.21 = (f32[8,1,256]{2,1,0:T(1,128)S(1)}, f32[8,1,256]{2,1,0:T(1,128)}, u32[]{:S(2)}) copy-start(f32[8,1,256]{2,1,0:T(1,128)} %copy-done.20) | copy-start | bytes 24580
  430.4 318.7 %copy-start.26 = (f32[3,768]{1,0:T(4,128)S(1)}, f32[3,768]{1,0:T(4,128)}, u32[]{:S(2)}) copy-start(f32[3,768]{1,0:T(4,128)} %copy-done.25) | copy-start | bytes 27652
  749.2 10.4 copy-start.1
  749.2 10.6 copy-start.4
  749.2 10.6 copy-start.6
  759.5 522.9 %reduce-scatter.10.cloned.1.call-start = ((), (), s32[]{:S(2)}) async-start(), calls=%async_computation.15 | async-start | bytes 2359296 | tf_op jit(solution)/shard_map/reduce_scatter | solution.py:63
  771.0 10.4 copy-start.13
  771.0 566.1 %reduce-scatter.14.cloned.1.call-start = ((), (), s32[]{:S(2)}) async-start(), calls=%async_computation.17 | async-start | bytes 4718592 | tf_op jit(solution)/shard_map/reduce_scatter | solution.py:67
  781.0 610.8 %reduce-scatter.8.cloned.1.call-start = ((), (), s32[]{:S(2)}) async-start(), calls=%async_computation.14 | async-start | bytes 4718592 | tf_op jit(solution)/shard_map/reduce_scatter | solution.py:63
  793.0 718.2 %reduce-scatter.20.cloned.1.call-start = ((), (), s32[]{:S(2)}) async-start(), calls=%async_computation.20 | async-start | bytes 18874368 | tf_op jit(solution)/shard_map/reduce_scatter | solution.py:67
  821.6 808.9 %reduce-scatter.18.cloned.1.call-start = ((), (), s32[]{:S(2)}) async-start(), calls=%async_computation.19 | async-start | bytes 18874368 | tf_op jit(solution)/shard_map/reduce_scatter | solution.py:63
  855.7 894.1 %reduce-scatter.16.cloned.1.call-start = ((), (), s32[]{:S(2)}) async-start(), calls=%async_computation.18 | async-start | bytes 18874368 | tf_op jit(solution)/shard_map/reduce_scatter | solution.py:63
  887.8 306.0 %copy-start.2 = (bf16[3,768,512]{1,2,0:T(8,128)(2,1)S(1)}, bf16[3,768,512]{1,2,0:T(8,128)(2,1)}, u32[]{:S(2)}) copy-start(bf16[3,768,512]{1,2,0:T(8,128)(2,1)} %copy-done.1) | copy-start | bytes 7077892
  1193.8 21.5 %copy-start.24 = (f32[3,768]{1,0:T(4,128)S(1)}, f32[3,768]{1,0:T(4,128)}, u32[]{:S(2)}) copy-start(f32[3,768]{1,0:T(4,128)} %copy-done.23) | copy-start | bytes 27652
  1193.8 21.5 %copy-start.22 = (f32[8,1,256]{2,1,0:T(1,128)S(1)}, f32[8,1,256]{2,1,0:T(1,128)}, u32[]{:S(2)}) copy-start(f32[8,1,256]{2,1,0:T(1,128)} %copy-done.20) | copy-start | bytes 24580
  1193.8 21.5 %copy-start.27 = (f32[3,768]{1,0:T(4,128)S(1)}, f32[3,768]{1,0:T(4,128)}, u32[]{:S(2)}) copy-start(f32[3,768]{1,0:T(4,128)} %copy-done.25) | copy-start | bytes 27652
  (6 other events, 11.9 us)
Sparse Core Ops, SparseCore 0:
  10.4 25.9 all-gather.10
  38.3 23.0 all-gather.12
  63.9 27.8 all-gather.8
  93.5 27.8 all-gather.14
  123.1 55.4 all-gather.20
  180.4 53.8 all-gather.18
  236.2 53.8 all-gather.16
  415.4 778.3 all-reduce.8
  1197.6 39.9 reduce-scatter.11
  1241.3 40.9 reduce-scatter.9
  1286.3 50.7 reduce-scatter.13
  1340.9 50.7 reduce-scatter.7
  1395.9 115.2 reduce-scatter.19
  1515.2 115.2 reduce-scatter.17
  1634.5 115.2 reduce-scatter.15
where the time goes:
time: 1760 us
  waiting for transfers between devices  879 us (50%)
  matrix products  448 us (25%)
  blocking collectives  341 us (19%)
  other arithmetic  54 us (3%)
  local copies, waits for them, and re-layouts  17.6 us (1%)
    dot_general x21, matrix products, matmul_f32(): return jnp.einsum(form, left, right, preferred_element_type=jnp.float32)  394 us
    psum x1, blocking collectives, device_step(): lax.psum(jnp.concatenate([dk_part, dv_part], axis=-1).astype(jnp.float32)...  316 us
    reduce_scatter x5, waiting for transfers between devices, scatter_rows(): return lax.psum_scatter(grad_full, 'fsdp', scatter_dimension=0, tiled=True)  312 us
    psum x1, waiting for transfers between devices, device_step(): branch_sum = lax.psum(branch_part, 'tp')  295 us
    reduce_scatter x2, waiting for transfers between devices, scatter_cols(): return lax.psum_scatter(grad_full, 'fsdp', scatter_dimension=1, tiled=True)  174 us
    all_gather x5, waiting for transfers between devices, gather_rows(): return lax.all_gather(w_part, 'fsdp', axis=0, tiled=True)  95.1 us
  transfers between devices with their start and end apart: 15, of which 12 were waited for; matrix products, arithmetic and copies ran while one was open for 22% of the time, Pallas kernels for 0%

commit v1 on v0

v1 whole, which is shorter than its diff:
```python
import functools
import math
import jax
import jax.numpy as jnp
from jax import lax
from jax.experimental import pallas as pl
from jax.experimental.pallas import tpu as pltpu
from jax.sharding import PartitionSpec as P

F32 = jnp.float32
BF16 = jnp.bfloat16
WIRE = jnp.bfloat16
STEP = 32
ZERO, ONE, TWO, THREE = range(4)


def rope_tables(seq_len, head_dim):
    half_dim = head_dim // 2
    inv_freq = jnp.power(10000.0, -2.0 * jnp.arange(half_dim, dtype=F32) / head_dim)
    angle = jnp.arange(seq_len, dtype=F32)[:, None] * inv_freq[None, :]
    return jnp.cos(angle), jnp.sin(angle)


def row_loop(rows, fn):
    def body(i, carry):
        fn(pl.ds(pl.multiple_of(i * STEP, STEP), STEP))
        return carry

    lax.fori_loop(0, rows // STEP, body, 0)


def contract(left, right, dims):
    return lax.dot_general(left, right, ((dims[:1], dims[1:]), ((), ())), preferred_element_type=F32)


def front_kernel(dims, x, dy, gain, sq, skv, sg, su, sod,
                 wcat, wkv, wod, gain_all, h, qkv, gate, up, act, datt, dact,
                 hv, wv, wodv, wqv, xt, yt, gt, et, b_q, b_kv, b_g, b_od, b_u, gv,
                 load, wload, keep, bsem, gsem, gain_s, gain_r, send, recv):
    rt_rows, col = dims
    tok, width = x.shape
    inner, kv, ff = sq.shape[ONE], skv.shape[ONE], sg.shape[ONE]
    blk = sq.shape[ZERO]
    ka = inner + ff
    n = tok // rt_rows
    me = lax.axis_index('fsdp')

    def local(src, dst, sem):
        return pltpu.make_async_copy(src, dst, sem)

    def remote(src, dst, s, r, to):
        return pltpu.make_async_remote_copy(src_ref=src, dst_ref=dst, send_sem=s, recv_sem=r, device_id={'fsdp': me ^ to},
                                            device_id_type=pl.DeviceIdType.MESH)

    items = (
        (sq, wcat, TWO * ff, inner), (skv, wkv, ZERO, kv), (sg, wcat, ZERO, ff), (sod, wod, ZERO, blk), (su, wcat, ff, ff),
    )

    def block(i, mask, part=None):
        _, full, at, wide = items[i]
        at_blk = pl.multiple_of((me ^ mask) * blk, blk)
        if i == THREE:
            rows = pl.ds(ZERO, ka) if part is None else pl.ds(part * (ka // TWO), ka // TWO)
            return full.at[rows, pl.ds(at_blk, blk)]
        rows = pl.ds(at_blk, blk) if part is None else pl.ds(at_blk + part * (blk // TWO), blk // TWO)
        return full.at[rows, pl.ds(at, wide)]

    def own_to(i, to, num):
        return remote(items[i][ZERO], block(i, ZERO), send.at[i, num], recv.at[i, num], to)

    def pass_to(i, mask, to, num, part=None):
        return remote(block(i, mask, part), block(i, mask, part), send.at[i, num], recv.at[i, num], to)

    def arrived(i, mask, to, num, part=None):
        remote(block(i, mask, part), block(i, mask, part), send.at[i, num], recv.at[i, num], to).wait_recv()

    def depart(i):
        own_to(i, TWO, ZERO).start()
        own_to(i, 4, ONE).start()
        own_to(i, ONE, 4).start()

    def relay(i):
        arrived(i, TWO, TWO, ZERO)
        pass_to(i, TWO, 4, TWO, ZERO).start()
        arrived(i, 4, 4, ONE)
        pass_to(i, 4, TWO, THREE, ONE).start()
        pass_to(i, TWO, ONE, 5).start()
        pass_to(i, 4, ONE, 6).start()

    def corner(i):
        arrived(i, 6, 4, TWO, ZERO)
        pass_to(i, 6, ONE, 7, ZERO).start()
        arrived(i, 6, TWO, THREE, ONE)
        pass_to(i, 6, ONE, 8, ONE).start()

    def full(i):
        arrived(i, ONE, ONE, 4)
        arrived(i, THREE, ONE, 5)
        arrived(i, 5, ONE, 6)
        arrived(i, 7, ONE, 7, ZERO)
        arrived(i, 7, ONE, 8, ONE)

    def sent(i):
        own_to(i, TWO, ZERO).wait_send()
        own_to(i, 4, ONE).wait_send()
        own_to(i, ONE, 4).wait_send()
        pass_to(i, TWO, 4, TWO, ZERO).wait_send()
        pass_to(i, 4, TWO, THREE, ONE).wait_send()
        pass_to(i, TWO, ONE, 5).wait_send()
        pass_to(i, 4, ONE, 6).wait_send()
        pass_to(i, 6, ONE, 7, ZERO).wait_send()
        pass_to(i, 6, ONE, 8, ONE).wait_send()

    bounce = (b_q, b_kv, b_g, b_od, b_u)

    def own_in(i):
        return local(items[i][ZERO], bounce[i], bsem.at[i])

    def own_out(i):
        return local(bounce[i], block(i, ZERO), bsem.at[i])

    def tile_rows(k):
        return pl.ds(pl.multiple_of(k * rt_rows, rt_rows), rt_rows)

    def tiles(fn):
        def body(k, carry):
            fn(k)
            return carry

        lax.fori_loop(ZERO, n, body, ZERO)

    def dot_cols(left, weight, dims_, out, wide, at=ZERO):
        def body(j, carry):
            cs = pl.ds(pl.multiple_of(j * col, col), col)
            rhs = weight[:, cs] if dims_[ONE] == ZERO else weight[cs, :]
            out[:, pl.ds(pl.multiple_of(at + j * col, col), col)] = contract(left[...], rhs, dims_).astype(BF16)
            return carry

        lax.fori_loop(ZERO, wide // col, body, ZERO)

    def gain_cols(mask):
        return pl.ds(pl.multiple_of((me ^ mask) * blk, blk), blk)

    def gain_to(m):
        return remote(gain, gain_all.at[:, gain_cols(ZERO)], gain_s.at[m - ONE], gain_r.at[m - ONE], m)

    def gain_from(m):
        return remote(gain, gain_all.at[:, gain_cols(m)], gain_s.at[m - ONE], gain_r.at[m - ONE], m)

    def gain_in(m):
        return local(gain if m == ZERO else gain_all.at[:, gain_cols(m)], gv.at[:, gain_cols(m)], gsem.at[m])

    peers = range(ONE, 8)
    for m in peers:
        gain_to(m).start()
    for i in range(THREE):
        depart(i)
    gain_in(ZERO).start()
    for i in range(5):
        own_in(i).start()
    for m in peers:
        gain_from(m).wait_recv()
        gain_in(m).start()
    for i in range(5):
        own_in(i).wait()
        own_out(i).start()
    for m in range(8):
        gain_in(m).wait()

    def x_load(k):
        return local(x.at[tile_rows(k)], xt.at[lax.rem(k, TWO)], load.at[lax.rem(k, TWO)])

    def h_keep(k):
        return local(hv.at[tile_rows(k)], h.at[tile_rows(k)], keep.at[lax.rem(k, TWO)])

    x_load(ZERO).start()

    def norm(k):
        x_load(k).wait()

        @pl.when(k + ONE < n)
        def _():
            x_load(k + ONE).start()

        def rows(sl):
            xv = xt[lax.rem(k, TWO), sl, :].astype(F32)
            cent = xv - jnp.mean(xv, axis=-ONE, keepdims=True)
            inv = lax.rsqrt(jnp.mean(cent * cent, axis=-ONE, keepdims=True) + 1e-5)
            hv[pl.ds(pl.multiple_of(k * rt_rows + sl.start, STEP), STEP), :] = (cent * inv * gv[ZERO:ONE, :]).astype(BF16)

        row_loop(rt_rows, rows)

        @pl.when(k >= TWO)
        def _():
            h_keep(k - TWO).wait()

        h_keep(k).start()

    tiles(norm)
    h_keep(n - TWO).wait()
    h_keep(n - ONE).wait()

    for i in range(THREE):
        relay(i)
    depart(THREE)
    for i in range(TWO):
        corner(i)
    for i in range(5):
        own_out(i).wait()
    for i in range(TWO):
        full(i)
    w0 = local(wcat.at[:, pl.ds(TWO * ff, inner)], wqv.at[:, pl.ds(ZERO, inner)], wload.at[ZERO])
    w1 = local(wkv, wqv.at[:, pl.ds(inner, kv)], wload.at[ONE])
    w0.start()
    w1.start()
    w0.wait()
    w1.wait()

    def out_keep(k, src, dst, which):
        return local(src, dst.at[tile_rows(k)], keep.at[which])

    def qkv_tile(k):
        @pl.when(k >= ONE)
        def _():
            out_keep(k - ONE, yt.at[:, pl.ds(ZERO, inner + kv)], qkv, TWO).wait()

        dot_cols(hv.at[tile_rows(k)], wqv, (ONE, ZERO), yt, inner + kv)
        out_keep(k, yt.at[:, pl.ds(ZERO, inner + kv)], qkv, TWO).start()

    tiles(qkv_tile)
    out_keep(n - ONE, yt.at[:, pl.ds(ZERO, inner + kv)], qkv, TWO).wait()

    corner(TWO)
    full(TWO)
    w2 = local(wcat.at[:, pl.ds(ZERO, ff)], wv, wload.at[TWO])
    w2.start()
    w2.wait()

    def gate_tile(k):
        @pl.when(k >= ONE)
        def _():
            out_keep(k - ONE, yt.at[:, pl.ds(ZERO, ff)], gate, TWO).wait()

        dot_cols(hv.at[tile_rows(k)], wv, (ONE, ZERO), yt, ff)
        out_keep(k, yt.at[:, pl.ds(ZERO, ff)], gate, TWO).start()

    tiles(gate_tile)
    out_keep(n - ONE, yt.at[:, pl.ds(ZERO, ff)], gate, TWO).wait()

    def dy_load(k):
        return local(dy.at[tile_rows(k)], xt.at[lax.rem(k, TWO)], load.at[lax.rem(k, TWO)])

    dy_load(ZERO).start()
    relay(THREE)
    depart(4)
    corner(THREE)
    full(THREE)
    w3 = local(wod, wodv, wload.at[THREE])
    w3.start()
    w3.wait()

    def back_keeps(k):
        return (local(yt.at[:, pl.ds(ZERO, inner)], datt.at[tile_rows(k)], keep.at[TWO]),
                local(yt.at[:, pl.ds(inner, ff)], dact.at[tile_rows(k)], keep.at[THREE]))

    def back_tile(k):
        dy_load(k).wait()

        @pl.when(k + ONE < n)
        def _():
            dy_load(k + ONE).start()

        @pl.when(k == (TWO * n) // THREE)
        def _():
            relay(4)

        @pl.when(k >= ONE)
        def _():
            for c in back_keeps(k - ONE):
                c.wait()

        dot_cols(xt.at[lax.rem(k, TWO)], wodv, (ONE, ONE), yt, ka)
        for c in back_keeps(k):
            c.start()

    tiles(back_tile)
    for c in back_keeps(n - ONE):
        c.wait()

    def gate_load(k):
        return local(gate.at[tile_rows(k)], gt, load.at[TWO])

    gate_load(ZERO).start()
    corner(4)
    full(4)
    w4 = local(wcat.at[:, pl.ds(ff, ff)], wv, wload.at[4])
    w4.start()
    w4.wait()

    def up_keeps(k):
        return (local(yt.at[:, pl.ds(ZERO, ff)], up.at[tile_rows(k)], keep.at[TWO]), local(et, act.at[tile_rows(k)], keep.at[THREE]))

    def up_tile(k):
        @pl.when(k >= ONE)
        def _():
            for c in up_keeps(k - ONE):
                c.wait()

        dot_cols(hv.at[tile_rows(k)], wv, (ONE, ZERO), yt, ff)
        gate_load(k).wait()

        def rows(sl):
            g = gt[sl, :].astype(F32)
            et[sl, :] = (g * jax.nn.sigmoid(g) * yt[sl, ZERO:ff].astype(F32)).astype(BF16)

        row_loop(rt_rows, rows)

        @pl.when(k + ONE < n)
        def _():
            gate_load(k + ONE).start()

        for c in up_keeps(k):
            c.start()

    tiles(up_tile)
    for c in up_keeps(n - ONE):
        c.wait()
    for i in range(5):
        sent(i)
    for m in peers:
        gain_to(m).wait_send()
    g_out = local(gv.at[:, gain_cols(ZERO)], gain_all.at[:, gain_cols(ZERO)], gsem.at[ZERO])
    g_out.start()
    g_out.wait()


def front_call(x, dy, gain, sq, skv, sg, su, sod, rt_rows=384, col=512):
    tok, width = x.shape
    inner, kv, ff = sq.shape[1], skv.shape[1], sg.shape[1]
    blk = sq.shape[0]
    ka = inner + ff
    shape = jax.ShapeDtypeStruct
    outs = (
        shape((width, 2 * ff + inner), BF16), shape((width, kv), BF16), shape((ka, width), BF16), shape((8, width), F32),
        shape((tok, width), BF16), shape((tok, inner + kv), BF16), shape((tok, ff), BF16), shape((tok, ff), BF16), shape((tok, ff), BF16),
        shape((tok, inner), BF16), shape((tok, ff), BF16),
    )
    sems = pltpu.SemaphoreType.DMA
    scratch = [
        pltpu.VMEM((tok, width), BF16), pltpu.VMEM((width, ff), BF16), pltpu.VMEM((ka, width), BF16), pltpu.VMEM((width, inner + kv), BF16),
        pltpu.VMEM((2, rt_rows, width), BF16), pltpu.VMEM((rt_rows, max(ka, inner + kv)), BF16), pltpu.VMEM((rt_rows, ff), BF16),
        pltpu.VMEM((rt_rows, ff), BF16), pltpu.VMEM(sq.shape, BF16), pltpu.VMEM(skv.shape, BF16), pltpu.VMEM(sg.shape, BF16), pltpu.VMEM(sod.shape, BF16), pltpu.VMEM(su.shape, BF16),
        pltpu.VMEM((8, width), F32),
        sems((3,)), sems((5,)), sems((4,)), sems((5,)), sems((8,)), sems((7,)), sems((7,)), sems((5, 9)), sems((5, 9)),
    ]
    flops = 2 * tok * width * (2 * ka + ff + kv)
    anywhere = pl.BlockSpec(memory_space=pl.ANY)
    return pl.pallas_call(
        functools.partial(front_kernel, (rt_rows, col)),
        out_shape=outs,
        in_specs=[anywhere] * 8,
        out_specs=tuple(anywhere for _ in outs),
        scratch_shapes=scratch,
        cost_estimate=pl.CostEstimate(flops=flops, bytes_accessed=150_000_000, transcendentals=tok * ff),
        compiler_params=pltpu.CompilerParams(vmem_limit_bytes=67_000_000, has_side_effects=True),
        name='forward',
    )(x, dy, gain, sq, skv, sg, su, sod)


def back_kernel(dims, att, act, wod, gate, up, dact, dq, wcat, wkv, dkv, table, h, dy, x, gain,
                y_out, gx_out, part, line, kvline, dcat, dhkv, peer_a, peer_b, own_a, own_b, got_a, got_b, gsum, gtmp, kvsum, snd_a, snd_b,
                wa, wb, st, wv, tv, ctile, gt, ot, rt, sa, sb, zr, zo, zs, zx, zd, zk, kr, ko, kz, gv, kw, gw,
                load, wload, wait_y, zload, zstore, kstore, rs_s, rs_r, kv_s, kv_r, ag_s, ag_r, core_s, core_r, far_s, far_r, own_s, put_s, kf_s, kf_r, kf_l, gl_s, gf_s, gf_r, gz_s, gz_r):
    nc, cr, col, tile = dims
    tok, width = h.shape
    inner, ff = att.shape[ONE], act.shape[ONE]
    ka, kb = inner + ff, wcat.shape[ONE]
    kv = dkv.shape[ONE]
    head = kv // TWO
    n_pos = table.shape[ZERO]
    rt_rows = 4 * cr
    blk = width // 8
    mid = width // TWO
    na, nb = ka // tile, (kb + kv) // tile
    depth = THREE
    last = THREE
    hop_lag = TWO
    end = TWO * nc - ONE + hop_lag * (last + TWO)
    me = lax.axis_index('fsdp')
    z = lax.axis_index('tp')

    def remote(src, dst, send, recv, **to):
        return pltpu.make_async_remote_copy(src_ref=src, dst_ref=dst, send_sem=send, recv_sem=recv,
                                            device_id=to, device_id_type=pl.DeviceIdType.MESH)

    def local(src, dst, sem):
        return pltpu.make_async_copy(src, dst, sem)

    def chunk_row(d, c):
        return pl.multiple_of(lax.rem(c, nc) * (TWO * cr) + d * cr, cr)

    def chunk_rows(d, c):
        return pl.ds(chunk_row(d, c), cr)

    def slot_parts(t):
        parts = []
        up_z, down_z = lax.rem(z + ONE, last + ONE), lax.rem(z + last, last + ONE)
        for d in range(TWO):
            parts.append(line_parts(t, d, up_z, down_z))
        return parts

    def line_parts(t, d, up_z, down_z):
        if True:
            rank = z if d == ZERO else last - z
            fwd, back = (up_z, down_z) if d == ZERO else (down_z, up_z)

            def hop(c, src=None):
                src = part.at[lax.div(c, nc), chunk_rows(d, c)] if src is None else src
                return remote(src, line.at[d, c], rs_s.at[d, c], rs_r.at[d, c], tp=fwd)

            def mid_hop(c):
                return hop(c, zs.at[d, lax.rem(c, depth)])

            def kv_hop(c, src=None):
                src = dkv.at[chunk_rows(d, c)] if src is None else src
                return remote(src, kvline.at[d, c], kv_s.at[d, c], kv_r.at[d, c], tp=fwd)

            def mid_kv_hop(c):
                return kv_hop(c, kz.at[d, lax.rem(c, depth)])

            def bcast_of(c, dst, src=None):
                src = dst.at[chunk_rows(d, c)] if src is None else src
                return remote(src, dst.at[chunk_rows(d, c)], ag_s.at[d, c], ag_r.at[d, c], tp=back)

            def keep_of(c, dst):
                return local(zs.at[d, lax.rem(c, depth)], dst.at[chunk_rows(d, c)], zstore.at[d, lax.rem(c, depth)])

            def for_kind(c, fn):
                @pl.when(c < nc)
                def _():
                    fn(y_out)

                @pl.when(c >= nc)
                def _():
                    fn(gx_out)

            def depart():
                @pl.when((rank == ZERO) & (t >= ZERO) & (t < TWO * nc))
                def _():
                    hop(t).start()

                    @pl.when(t < nc)
                    def _():
                        kv_hop(t).start()

            c = t - hop_lag * rank
            rows = chunk_rows(d, c)
            own = pl.ds(pl.multiple_of(lax.rem(c, nc) * cr, cr), cr)

            def load_of(i):
                return (
                    local(part.at[lax.div(c, nc), rows], zo.at[d], zload.at[d, ZERO]), local(line.at[d, c], zr.at[d], zload.at[d, ONE]),
                    local(x.at[rows], zx, zload.at[d, TWO]), local(dy.at[rows], zd, zload.at[d, THREE]),
                    local(dhkv.at[own], zk, zload.at[d, 4]), local(dkv.at[rows], ko.at[d], zload.at[d, 5]),
                    local(kvline.at[d, lax.rem(c, nc)], kr.at[d], zload.at[d, 6]),
                )[i]

            busy = (rank > ZERO) & (c >= ZERO) & (c < TWO * nc)

            def begin():
                @pl.when(busy)
                def _():
                    load_of(ZERO).start()

                    @pl.when(rank == last)
                    def _():
                        load_of(TWO).start()

                        @pl.when(c >= nc)
                        def _():
                            load_of(THREE).start()

                    hop(c).wait_recv()
                    load_of(ONE).start()

                    @pl.when(c < nc)
                    def _():
                        load_of(5).start()
                        kv_hop(c).wait_recv()
                        load_of(6).start()

            def finish():
                @pl.when(busy & (rank < last))
                def _():
                    @pl.when(c >= depth)
                    def _():
                        mid_hop(c - depth).wait_send()

                    load_of(ZERO).wait()
                    load_of(ONE).wait()

                    def add(sl):
                        zs[d, lax.rem(c, depth), sl, :] = (zr[d, sl, :].astype(F32) + zo[d, sl, :].astype(F32)).astype(BF16)

                    row_loop(cr, add)
                    mid_hop(c).start()

                    @pl.when(c < nc)
                    def _():
                        @pl.when(c >= depth)
                        def _():
                            mid_kv_hop(c - depth).wait_send()

                        load_of(5).wait()
                        load_of(6).wait()
                        kz[d, lax.rem(c, depth)] = (kr[d].astype(F32) + ko[d].astype(F32)).astype(BF16)
                        mid_kv_hop(c).start()

                @pl.when(busy & (rank == last))
                def _():
                    @pl.when(c >= nc)
                    def _():
                        load_of(4).start()

                    @pl.when(c >= depth)
                    def _():
                        bcast_of(c - depth, y_out).wait_send()
                        keep_of(c - depth, y_out).wait()

                    load_of(ZERO).wait()
                    load_of(ONE).wait()
                    load_of(TWO).wait()

                    @pl.when(c < nc)
                    def _():
                        def fin(sl):
                            branch = zr[d, sl, :].astype(F32) + zo[d, sl, :].astype(F32)
                            zs[d, lax.rem(c, depth), sl, :] = (zx[sl, :].astype(F32) + branch).astype(BF16)

                        row_loop(cr, fin)

                    @pl.when(c >= nc)
                    def _():
                        load_of(THREE).wait()
                        load_of(4).wait()

                        def fin(sl):
                            dh = (zr[d, sl, :].astype(F32) + zo[d, sl, :].astype(F32) + zk[sl, :]).astype(BF16).astype(F32)
                            xv = zx[sl, :].astype(F32)
                            cent = xv - jnp.mean(xv, axis=-ONE, keepdims=True)
                            inv = lax.rsqrt(jnp.mean(cent * cent, axis=-ONE, keepdims=True) + 1e-5)
                            hat = cent * inv
                            gv[8:9, :] = gv[8:9, :] + jnp.sum(dh * hat, axis=ZERO, keepdims=True)
                            dn = dh * gv[ZERO:ONE, :]
                            dx = inv * (dn - jnp.mean(dn, axis=-ONE, keepdims=True)
                                        - hat * jnp.mean(dn * hat, axis=-ONE, keepdims=True))
                            zs[d, lax.rem(c, depth), sl, :] = (zd[sl, :].astype(F32) + dx).astype(BF16)

                        row_loop(cr, fin)

                    for_kind(c, lambda dst: keep_of(c, dst).start())
                    for_kind(c, lambda dst: bcast_of(c, dst, zs.at[d, lax.rem(c, depth)]).start())

                    @pl.when(c < nc)
                    def _():
                        load_of(5).wait()
                        load_of(6).wait()
                        pos = pl.ds(pl.multiple_of(lax.rem(chunk_row(d, c), n_pos), cr), cr)
                        cos_t, sin_t = tv[pos, ZERO:head // TWO], tv[pos, head // TWO:head]

                        def summed(lo, hi):
                            return (kr[d, :, lo:hi].astype(F32) + ko[d, :, lo:hi].astype(F32)).astype(BF16)

                        first = summed(ZERO, head // TWO).astype(F32)
                        second = summed(head // TWO, head).astype(F32)
                        kz[d, ZERO, :, ZERO:head // TWO] = (first * cos_t + second * sin_t).astype(BF16)
                        kz[d, ZERO, :, head // TWO:head] = (second * cos_t - first * sin_t).astype(BF16)
                        kz[d, ZERO, :, head:kv] = summed(head, kv)
                        keep_kv = local(kz.at[d, ZERO], dcat.at[rows, pl.ds(kb, kv)], kstore.at[ZERO])
                        keep_kv.start()

                        def cols(j, carry):
                            cs = pl.ds(pl.multiple_of(j * col, col), col)
                            zk[:, cs] = contract(kz[d, ZERO], wv[cs, :], (ONE, ONE))
                            return carry

                        lax.fori_loop(ZERO, width // col, cols, ZERO)
                        keep_h = local(zk, dhkv.at[own], kstore.at[ONE])
                        keep_h.start()
                        keep_kv.wait()
                        keep_h.wait()

            e = t - hop_lag * (last + ONE) - hop_lag * (TWO - rank)

            def pass_on():
                @pl.when(((rank == ONE) | (rank == TWO)) & (e >= ZERO) & (e < TWO * nc))
                def _():
                    bcast_of(e, y_out).wait_recv()
                    for_kind(e, lambda dst: bcast_of(e, dst).start())

            def settle():
                def each(c, carry):
                    tail = TWO * nc - depth
                    kv_tail = (c >= nc - depth) & (c < nc)

                    @pl.when(rank == ZERO)
                    def _():
                        hop(c).wait_send()
                        bcast_of(c, y_out).wait_recv()

                        @pl.when(c < nc)
                        def _():
                            kv_hop(c).wait_send()

                    @pl.when((rank == ONE) | (rank == TWO))
                    def _():
                        bcast_of(c, y_out).wait_send()

                        @pl.when(c >= tail)
                        def _():
                            mid_hop(c).wait_send()

                        @pl.when(kv_tail)
                        def _():
                            mid_kv_hop(c).wait_send()

                    @pl.when((rank == last) & (c >= tail))
                    def _():
                        bcast_of(c, y_out).wait_send()
                        keep_of(c, y_out).wait()

                    return carry

                lax.fori_loop(ZERO, TWO * nc, each, ZERO)

            return depart, begin, finish, pass_on, settle

    def slot(t):
        parts = slot_parts(t)
        for i in range(4):
            for p in parts:
                p[i]()

        @pl.when(t == end)
        def _():
            for p in parts:
                p[4]()

    def gain_total():
        low = pl.ds(8, 8)
        which = lax.div(z, last)

        def cols(mask):
            return pl.ds(pl.multiple_of((me ^ mask) * blk, blk), blk)

        def plane(m):
            return remote(gv.at[low, cols(m)], gtmp.at[m], gf_s.at[m], gf_r.at[m], fsdp=me ^ m)

        def along(i):
            return remote(gw.at[ZERO], gsum.at[which], gz_s.at[i], gz_r.at[which], tp=lax.rem(z + ONE + i, last + ONE))

        def arrived(w):
            remote(gw.at[ZERO], gsum.at[w], gz_s.at[ZERO], gz_r.at[w], tp=lax.rem(z + ONE, last + ONE)).wait_recv()

        peers = range(ONE, 8)

        @pl.when((z == ZERO) | (z == last))
        def _():
            for m in peers:
                plane(m).start()
            own = local(gv.at[low, cols(ZERO)], gw.at[ZERO], gl_s.at[ZERO])
            own.start()
            for m in peers:
                plane(m).wait_recv()
                local(gtmp.at[m], gw.at[m], gl_s.at[m]).start()
            own.wait()
            for m in peers:
                local(gtmp.at[m], gw.at[m], gl_s.at[m]).wait()
            gw[ZERO] = jnp.sum(gw[...], axis=ZERO)
            home = local(gw.at[ZERO], gsum.at[which], gl_s.at[ZERO])
            home.start()
            for i in range(THREE):
                along(i).start()
            home.wait()
            for m in peers:
                plane(m).wait_send()

        @pl.when(z != ZERO)
        def _():
            arrived(ZERO)

        @pl.when(z != last)
        def _():
            arrived(ONE)

        @pl.when((z == ZERO) | (z == last))
        def _():
            for i in range(THREE):
                along(i).wait_send()

    def tile_rows(k):
        return pl.ds(pl.multiple_of(k * rt_rows, rt_rows), rt_rows)

    def y_step(k):
        srcs = [local(att.at[tile_rows(k)], ctile.at[:, pl.ds(ZERO, inner)], load.at[ZERO]),
                local(act.at[tile_rows(k)], ctile.at[:, pl.ds(inner, ff)], load.at[ONE])]
        for s in srcs:
            s.start()
        for s in srcs:
            s.wait()

        def cols(j, carry):
            cs = pl.ds(pl.multiple_of(j * col, col), col)
            gt[:, cs] = contract(ctile[:, ZERO:ka], wa[ZERO:ka, cs], (ONE, ZERO)).astype(BF16)
            return carry

        lax.fori_loop(ZERO, width // col, cols, ZERO)
        dst = local(gt.at[:, pl.ds(ZERO, width)], part.at[ZERO, tile_rows(k)], wait_y)
        dst.start()
        dst.wait()

    def h_step(k):
        rows = tile_rows(k)
        srcs = [local(gate.at[rows], gt.at[:, pl.ds(ZERO, ff)], load.at[ZERO]), local(up.at[rows], ctile.at[:, pl.ds(ZERO, ff)], load.at[ONE]),
                local(dact.at[rows], ctile.at[:, pl.ds(ff, ff)], load.at[TWO]), local(dq.at[rows], ctile.at[:, pl.ds(TWO * ff, kb - TWO * ff)], load.at[THREE])]
        for s in srcs:
            s.start()
        for s in srcs:
            s.wait()

        def act_back(sl):
            g = gt[sl, ZERO:ff].astype(F32)
            u = ctile[sl, ZERO:ff].astype(F32)
            d_act = ctile[sl, ff:TWO * ff].astype(F32)
            sig = jax.nn.sigmoid(g)
            ctile[sl, ZERO:ff] = (d_act * u * (sig + g * sig * (1.0 - sig))).astype(BF16)
            ctile[sl, ff:TWO * ff] = (d_act * (g * sig)).astype(BF16)

        row_loop(rt_rows, act_back)
        keep = local(ctile, dcat.at[rows, pl.ds(ZERO, kb)], load.at[4])
        keep.start()

        def cols(j, carry):
            cs = pl.ds(pl.multiple_of(j * col, col), col)
            gt[:, cs] = contract(ctile[...], wb[cs, ZERO:kb], (ONE, ONE)).astype(BF16)
            return carry

        lax.fori_loop(ZERO, width // col, cols, ZERO)
        dst = local(gt.at[:, pl.ds(ZERO, width)], part.at[ONE, rows], wait_y)
        dst.start()
        dst.wait()
        keep.wait()

    def out_weights():
        return local(wod, wa.at[pl.ds(ZERO, ka)], wload.at[ZERO])

    def in_weights():
        return local(wcat, wb.at[pl.ds(ZERO, width), pl.ds(ZERO, kb)], wload.at[10])

    def operand(src):
        cps = []
        for q in range(8):
            mask = TWO * (q % 4) + q // 4
            cols = pl.ds(pl.multiple_of((me ^ mask) * blk, blk), blk)
            cps.append(local(src.at[:, cols], wa.at[pl.ds(ZERO, tok), pl.ds(q * blk, blk)], wload.at[q]))
        for c in cps:
            c.start()
        for c in cps:
            c.wait()

    first_b = -(-nb // TWO)

    def strip(is_a, k):
        if is_a:
            return k
        return jnp.where(k < first_b, k, jnp.where(k == first_b, nb - ONE, k - ONE))

    def wide_start(is_a, k):
        dst = st.at[lax.rem(k, TWO)]
        sem = wload.at[8 + lax.rem(k, TWO)]
        if is_a:
            @pl.when(k == ZERO)
            def _():
                local(att, dst, sem).start()

            @pl.when(k > ZERO)
            def _():
                local(act.at[:, pl.ds(pl.multiple_of((k - ONE) * tile, tile), tile)], dst, sem).start()
        else:
            local(dcat.at[:, pl.ds(pl.multiple_of(strip(is_a, k) * tile, tile), tile)], dst, sem).start()

    def wide(is_a, k, hi):
        local(dcat.at[:, pl.ds(ZERO, tile)], st.at[lax.rem(k, TWO)], wload.at[8 + lax.rem(k, TWO)]).wait()

        @pl.when(k + ONE < hi)
        def _():
            wide_start(is_a, k + ONE)

    def prod(is_a, k, odd):
        half = pl.ds(odd * mid, mid)
        if is_a:
            return contract(st[lax.rem(k, TWO)], wa[ZERO:tok, half], (ZERO, ZERO))
        return contract(wa[ZERO:tok, half], st[lax.rem(k, TWO)], (ZERO, ZERO))

    def place(ref, is_a, k):
        par = pl.multiple_of(lax.rem(k, TWO) * tile, tile)
        return ref.at[pl.ds(par, tile), :] if is_a else ref.at[:, pl.ds(par, tile)]

    def whole(ref, is_a, k):
        cs = pl.ds(pl.multiple_of(strip(is_a, k) * tile, tile), tile)
        return ref.at[cs, :] if is_a else ref.at[:, cs]

    def piece(ref, is_a, q):
        return ref.at[:, pl.ds(q * blk, blk)] if is_a else ref.at[pl.ds(q * blk, blk), :]

    def away(is_a, k, q):
        base, snd, got = (ZERO, snd_a, got_a) if is_a else (na, snd_b, got_b)
        return remote(whole(snd.at[q], is_a, k), whole(got.at[q], is_a, k), far_s.at[q, base + k], far_r.at[q, base + k],
                      fsdp=me ^ (TWO * (q + ONE)))

    def odd_steps(is_a, lo, hi, stop):
        base = ZERO if is_a else na
        peer = peer_a if is_a else peer_b

        def send(k):
            return remote(place(ot, is_a, k), whole(peer, is_a, k), core_s.at[base + k], core_r.at[base + k], fsdp=me ^ ONE)

        def one(k, carry):
            wide(is_a, k, hi)

            @pl.when(k >= stop[ZERO] + TWO)
            def _():
                send(k - TWO).wait_send()

            place(ot, is_a, k)[...] = prod(is_a, k, ONE)
            send(k).start()

            @pl.when(k == stop[ONE] - ONE)
            def _():
                send(k - ONE).wait_send()
                send(k).wait_send()

            return carry

        wide_start(is_a, lo)
        lax.fori_loop(lo, hi, one, ZERO)

    def even_steps(is_a, lo, hi, stop):
        base = ZERO if is_a else na
        peer, own, snd = (peer_a, own_a, snd_a) if is_a else (peer_b, own_b, snd_b)
        stage = sa if is_a else sb

        def take(k):
            return remote(place(ot, is_a, k), whole(peer, is_a, k), core_s.at[base + k], core_r.at[base + k], fsdp=me ^ ONE)

        def fetch(k):
            if not is_a:
                return [local(whole(peer, is_a, k), rt, own_s.at[TWO])]
            rows = pl.ds(pl.multiple_of(k * tile, tile), tile)
            return [local(peer.at[rows, pl.ds(i * tile, tile)], rt.at[pl.ds(i * tile, tile)], own_s.at[TWO + i])
                    for i in range(mid // tile)]

        def fetched():
            if not is_a:
                return rt[...]
            return jnp.concatenate([rt[i * tile:(i + ONE) * tile, :] for i in range(mid // tile)], axis=ONE)

        def mine(k):
            return local(piece(place(ot, is_a, k), is_a, ZERO), whole(own, is_a, k), own_s.at[lax.rem(k, TWO)])

        def put(k, q):
            return local(stage.at[lax.rem(k, TWO), q], whole(snd.at[q], is_a, k), put_s.at[lax.rem(k, TWO), q])

        def ship(k):
            for q in range(THREE):
                put(k, q).wait()
                away(is_a, k, q).start()

        def one(k, carry):
            take(k).wait_recv()
            for f in fetch(k):
                f.start()
            wide(is_a, k, hi)

            @pl.when(k >= stop[ZERO] + TWO)
            def _():
                mine(k - TWO).wait()

            acc = prod(is_a, k, ZERO)

            @pl.when(k >= stop[ZERO] + ONE)
            def _():
                ship(k - ONE)

            for f in fetch(k):
                f.wait()
            place(ot, is_a, k)[...] = acc + fetched()
            mine(k).start()
            for q in range(THREE):
                stage[lax.rem(k, TWO), q] = piece(place(ot, is_a, k), is_a, q + ONE)[...].astype(WIRE)
                put(k, q).start()

            @pl.when(k == stop[ONE] - ONE)
            def _():
                ship(k)
                mine(k - ONE).wait()
                mine(k).wait()

            return carry

        wide_start(is_a, lo)
        lax.fori_loop(lo, hi, one, ZERO)

    def far_wait(is_a, k):
        for q in range(THREE):
            away(is_a, k, q).wait_recv()

    def far_waits(is_a, but=-ONE):
        def one(k, carry):
            for q in range(THREE):
                away(is_a, k, q).wait_send()

            @pl.when(k != but)
            def _():
                far_wait(is_a, k)

            return carry

        lax.fori_loop(ZERO, na if is_a else nb, one, ZERO)

    def kv_send(i):
        which = lax.div(z, last)
        return remote(kw, kvsum.at[which], kf_s.at[i], kf_r.at[which], tp=lax.rem(z + ONE + i, last + ONE))

    def kv_total():
        @pl.when((z == ZERO) | (z == last))
        def _():
            k = first_b
            cs = pl.ds((nb - ONE) * tile, tile)
            far_wait(False, k)
            own_cp = local(own_b.at[:, cs], kw, load.at[ZERO])
            cps = [local(got_b.at[q, :, cs], sb.at[ZERO, q], load.at[ONE + q]) for q in range(THREE)]
            own_cp.start()
            for cp in cps:
                cp.start()
            own_cp.wait()
            for cp in cps:
                cp.wait()
            kw[...] = kw[...] + sb[ZERO, ZERO].astype(F32) + sb[ZERO, ONE].astype(F32) + sb[ZERO, TWO].astype(F32)
            home = local(kw, kvsum.at[lax.div(z, last)], kf_l)
            home.start()
            for i in range(THREE):
                kv_send(i).start()
            home.wait()

        @pl.when((z != ZERO) & (z != last))
        def _():
            far_wait(False, first_b)

    def kv_settle():
        def arrived(which):
            remote(kw, kvsum.at[which], kf_s.at[ZERO], kf_r.at[which], tp=lax.rem(z + ONE, last + ONE)).wait_recv()

        @pl.when(z != ZERO)
        def _():
            arrived(ZERO)

        @pl.when(z != last)
        def _():
            arrived(ONE)

        @pl.when((z == ZERO) | (z == last))
        def _():
            for i in range(THREE):
                kv_send(i).wait_send()

    out_weights().start()
    in_weights().start()
    gv[8:16, :] = jnp.zeros((8, width), F32)
    small = [local(gain, gv.at[pl.ds(ZERO, 8)], load.at[ZERO]), local(wkv, wv, load.at[ONE]), local(table, tv, load.at[TWO])]
    for s in small:
        s.start()

    ctile[:, ZERO:kv] = jnp.zeros((rt_rows, kv), BF16)
    blanks = [local(ctile.at[:, pl.ds(ZERO, kv)], dcat.at[pl.ds(i * rt_rows, rt_rows), pl.ds(kb, kv)], wload.at[TWO + i])
              for i in range(nc // TWO)]
    for s in blanks:
        s.start()
    for s in blanks + small:
        s.wait()

    steps = nc // TWO
    a_at, h_at, b_at = steps, steps + 4, TWO * steps + 4
    kv_at = b_at + 10
    per_a, per_b = -(-na // TWO), -(-first_b // TWO)

    def share(at, lo, hi, per, i):
        return jnp.minimum(lo + i * per, hi), jnp.minimum(lo + (i + ONE) * per, hi)

    def phase(s, at, n):
        return pl.when((s >= at) & (s < at + n))

    def step(s, carry):
        slot(s - ONE)

        @phase(s, ZERO, steps)
        def _():
            @pl.when(s == ZERO)
            def _():
                out_weights().wait()

            y_step(s)

        @phase(s, a_at, TWO)
        def _():
            @pl.when(s == a_at)
            def _():
                operand(dy)

            odd_steps(True, *share(s, ZERO, na, per_a, s - a_at), (ZERO, na))

        @phase(s, a_at + TWO, TWO)
        def _():
            even_steps(True, *share(s, ZERO, na, per_a, s - (a_at + TWO)), (ZERO, na))

        @phase(s, h_at, steps)
        def _():
            @pl.when(s == h_at)
            def _():
                in_weights().wait()

            h_step(s - h_at)

        for part_b in range(TWO):
            lo, hi = (ZERO, first_b) if part_b == ZERO else (first_b, nb)
            at = b_at + 4 * part_b

            @phase(s, at, TWO)
            def _():
                if part_b == ZERO:
                    @pl.when(s == at)
                    def _():
                        operand(h)

                odd_steps(False, *share(s, lo, hi, per_b, s - at), (lo, hi))

            @phase(s, at + TWO, TWO)
            def _():
                even_steps(False, *share(s, lo, hi, per_b, s - (at + TWO)), (lo, hi))

        @pl.when(s == kv_at)
        def _():
            kv_total()

        @pl.when(s == end - hop_lag * TWO + ONE)
        def _():
            gain_total()

        return carry

    lax.fori_loop(ZERO, end + TWO, step, ZERO)
    far_waits(True)
    far_waits(False, first_b)
    kv_settle()


def back_call(att, act, wod, gate, up, dact, dq, wcat, wkv, dkv, table, h, dy, x, gain, nc=12, col=512, tile=512):
    tok, width = h.shape
    inner, ff = att.shape[1], act.shape[1]
    ka, kb, kv = inner + ff, wcat.shape[1], dkv.shape[1]
    cr = tok // (2 * nc)
    rt_rows = 4 * cr
    blk, mid = width // 8, width // 2
    na, nb = ka // tile, (kb + kv) // tile
    big = max(mid, 2 * tile)
    shape = jax.ShapeDtypeStruct
    outs = (
        shape((tok, width), BF16), shape((tok, width), BF16), shape((2, tok, width), BF16), shape((2, 2 * nc, cr, width), BF16),
        shape((2, nc, cr, kv), BF16), shape((tok, kb + kv), BF16), shape((nc * cr, width), F32),
        shape((ka, mid), F32), shape((mid, kb + kv), F32), shape((ka, blk), F32), shape((blk, kb + kv), F32),
        shape((3, ka, blk), WIRE), shape((3, blk, kb + kv), WIRE), shape((2, 8, blk), F32), shape((8, 8, blk), F32), shape((2, blk, kv), F32),
        shape((3, ka, blk), WIRE), shape((3, blk, kb + kv), WIRE),
    )
    sems = pltpu.SemaphoreType.DMA
    scratch = [
        pltpu.VMEM((max(ka, tok), width), BF16), pltpu.VMEM((width, kb), BF16), pltpu.VMEM((2, tok, tile), BF16),
        pltpu.VMEM((width, kv), BF16), pltpu.VMEM(table.shape, F32),
        pltpu.VMEM((rt_rows, max(ka, kb)), BF16), pltpu.VMEM((rt_rows, max(ff, width)), BF16),
        pltpu.VMEM((big, big), F32), pltpu.VMEM((mid, tile), F32),
        pltpu.VMEM((2, 3, tile, blk), WIRE), pltpu.VMEM((2, 3, blk, tile), WIRE),
        pltpu.VMEM((2, cr, width), BF16), pltpu.VMEM((2, cr, width), BF16), pltpu.VMEM((2, 3, cr, width), BF16),
        pltpu.VMEM((cr, width), BF16), pltpu.VMEM((cr, width), BF16), pltpu.VMEM((cr, width), F32),
        pltpu.VMEM((2, cr, kv), BF16), pltpu.VMEM((2, cr, kv), BF16), pltpu.VMEM((2, 3, cr, kv), BF16),
        pltpu.VMEM((16, width), F32), pltpu.VMEM((blk, kv), F32), pltpu.VMEM((8, 8, blk), F32),
        sems((5,)), sems((11,)), sems, sems((2, 7)), sems((2, 3)), sems((2,)),
        sems((2, 2 * nc)), sems((2, 2 * nc)), sems((2, nc)), sems((2, nc)), sems((2, 2 * nc)), sems((2, 2 * nc)),
        sems((na + nb,)), sems((na + nb,)), sems((3, na + nb)), sems((3, na + nb)), sems((2 + mid // tile,)), sems((2, 3)),
        sems((3,)), sems((2,)), sems, sems((8,)), sems((8,)), sems((8,)), sems((3,)), sems((2,)),
    ]
    flops = 2 * tok * width * (2 * ka + 2 * kb)
    anywhere = pl.BlockSpec(memory_space=pl.ANY)
    return pl.pallas_call(
        functools.partial(back_kernel, (nc, cr, col, tile)),
        out_shape=outs,
        in_specs=[anywhere] * 15,
        out_specs=tuple(anywhere for _ in outs),
        scratch_shapes=scratch,
        cost_estimate=pl.CostEstimate(flops=2 * flops, bytes_accessed=200_000_000, transcendentals=tok * ff),
        compiler_params=pltpu.CompilerParams(vmem_limit_bytes=67_000_000, has_side_effects=True),
        name='backward',
    )(att, act, wod, gate, up, dact, dq, wcat, wkv, dkv, table, h, dy, x, gain)


def attention_kernel(heads, qkv, datt, table, att, dq, dkv, krot, dk_acc, dv_acc):
    n_pos = qkv.shape[0]
    head = qkv.shape[1] // (heads + 2)
    half = head // 2
    scale = 1.0 / math.sqrt(head)
    qb = 256

    def cos_of(sl):
        return table[sl, 0:half], table[sl, half:head]

    def turn(lo, sl, factor):
        cos_t, sin_t = cos_of(sl)
        first = qkv[sl, lo:lo + half].astype(F32)
        second = qkv[sl, lo + half:lo + head].astype(F32)
        return jnp.concatenate([(first * cos_t - second * sin_t) * factor, (second * cos_t + first * sin_t) * factor], axis=-1).astype(BF16)

    k_at, v_at = heads * head, (heads + 1) * head
    krot[...] = turn(k_at, slice(0, n_pos), 1.0)
    dk_acc[...] = jnp.zeros_like(dk_acc)
    dv_acc[...] = jnp.zeros_like(dv_acc)
    for r in range(heads):
        for i in range(n_pos // qb):
            sl = slice(i * qb, (i + 1) * qb)
            upto = (i + 1) * qb
            q = turn(r * head, sl, scale)
            k = krot[0:upto, :]
            v = qkv[0:upto, v_at:v_at + head]
            scores = contract(q, k, (1, 1))
            rows = lax.broadcasted_iota(jnp.int32, (qb, upto), 0) + i * qb
            scores = jnp.where(rows >= lax.broadcasted_iota(jnp.int32, (qb, upto), 1), scores, -1e30)
            exp_val = jnp.exp(scores - jnp.max(scores, axis=-1, keepdims=True))
            prob = exp_val / jnp.sum(exp_val, axis=-1, keepdims=True)
            prob_b = prob.astype(BF16)
            att[sl, r * head:(r + 1) * head] = contract(prob_b, v, (1, 0)).astype(BF16)
            do = datt[sl, r * head:(r + 1) * head]
            d_prob = contract(do, v, (1, 1)).astype(BF16).astype(F32)
            d_scores = (prob * (d_prob - jnp.sum(d_prob * prob, axis=-1, keepdims=True))).astype(BF16)
            d_rot = contract(d_scores, k, (1, 0)).astype(BF16).astype(F32) * scale
            cos_t, sin_t = cos_of(sl)
            first, second = d_rot[:, 0:half], d_rot[:, half:head]
            dq[sl, r * head:r * head + half] = (first * cos_t + second * sin_t).astype(BF16)
            dq[sl, r * head + half:(r + 1) * head] = (second * cos_t - first * sin_t).astype(BF16)
            dk_acc[0:upto, :] += contract(d_scores, q, (0, 0))
            dv_acc[0:upto, :] += contract(prob_b, do, (0, 0))
    dkv[:, 0:head] = dk_acc[...].astype(BF16)
    dkv[:, head:2 * head] = dv_acc[...].astype(BF16)


def attention_call(qkv, datt, table, n_batch):
    tok, wide = qkv.shape
    inner = datt.shape[1]
    head = table.shape[1]
    n_pos = tok // n_batch
    heads = inner // head

    def rows(n):
        return pl.BlockSpec((n_pos, n), lambda b: (b, 0))

    shape = jax.ShapeDtypeStruct
    flops = 2 * n_batch * heads * n_pos * n_pos * head * 7
    return pl.pallas_call(
        functools.partial(attention_kernel, heads),
        grid=(n_batch,),
        out_shape=(shape((tok, inner), BF16), shape((tok, inner), BF16), shape((tok, 2 * head), BF16)),
        in_specs=[rows(wide), rows(inner), pl.BlockSpec(table.shape, lambda b: (0, 0))],
        out_specs=(rows(inner), rows(inner), rows(2 * head)),
        scratch_shapes=[pltpu.VMEM((n_pos, head), BF16), pltpu.VMEM((n_pos, head), F32), pltpu.VMEM((n_pos, head), F32)],
        cost_estimate=pl.CostEstimate(flops=flops, bytes_accessed=20_000_000, transcendentals=n_batch * heads * n_pos * n_pos),
        compiler_params=pltpu.CompilerParams(vmem_limit_bytes=40_000_000),
        name='attention',
    )(qkv, datt, table)


def solution(mesh):
    def device_step(x_in, dy_out, ln_gain, w_q, w_k, w_v, w_o, w_gate, w_up, w_down):
        n_batch, seq_len, width = x_in.shape
        head_dim = w_k.shape[1]
        inner = w_q.shape[1]
        ff = w_gate.shape[1]
        tok = n_batch * seq_len
        x_rows = x_in.reshape(tok, width)
        dy = dy_out.reshape(tok, width)
        table = jnp.concatenate(rope_tables(seq_len, head_dim), axis=-1)

        gain8 = jnp.broadcast_to(ln_gain[None, :], (8, ln_gain.shape[0]))
        front = front_call(x_rows, dy, gain8, w_q, jnp.concatenate([w_k, w_v], axis=1), w_gate, w_up, jnp.concatenate([w_o, w_down], axis=0))
        wcat, wkv, wod, gain, h_norm, qkv, gate, up, act, d_att, d_act = front
        att, d_q, dkv = attention_call(qkv, d_att, table, n_batch)
        res = back_call(att, act, wod, gate, up, d_act, d_q, wcat, wkv, dkv, table, h_norm, dy, x_rows, gain)
        y_rows, gx_rows = res[0], res[1]
        own_a, own_b, got_a, got_b, gsum, _, kvsum = res[9:16]

        def total(own, got):
            return own + got[0].astype(F32) + got[1].astype(F32) + got[2].astype(F32)

        grad_od = total(own_a, got_a)
        big = 2 * ff + inner
        grad_in = total(own_b[:, :big], got_b[:, :, :big])
        grad_kv = kvsum[0] + kvsum[1]
        grad_gain = gsum[0, 0] + gsum[1, 0]
        return (y_rows.reshape(x_in.shape), gx_rows.reshape(x_in.shape), grad_gain, grad_in[:, 2 * ff:2 * ff + inner],
                grad_kv[:, :head_dim], grad_kv[:, head_dim:], grad_od[:inner], grad_in[:, :ff], grad_in[:, ff:2 * ff], grad_od[inner:])

    act_spec = P('fsdp', None, None)
    row_spec = P('fsdp', 'tp')
    kv_spec = P('fsdp', None)
    col_spec = P('tp', 'fsdp')
    in_specs = (act_spec, act_spec, P('fsdp'), row_spec, kv_spec, kv_spec, col_spec, row_spec, row_spec, col_spec)
    out_specs = (act_spec, act_spec, P('fsdp'), row_spec, kv_spec, kv_spec, col_spec, row_spec, row_spec, col_spec)
    return jax.shard_map(device_step, mesh=mesh, in_specs=in_specs, out_specs=out_specs, check_vma=False)
```

time: 1760 us -> 814 us (0.46)
  waiting for transfers between devices: 879 us -> 0 us
  Pallas kernels: 0 us -> 760 us
  matrix products: 448 us -> 0 us
  blocking collectives: 341 us -> 0 us
  other arithmetic: 54 us -> 13.1 us
  local copies, waits for them, and re-layouts: 17.6 us -> 37.7 us
    pallas_call x0 -> x3, Pallas kernels: none -> 760 us  [the longest x1 530 us: back_call(): pl.pallas_call(functools.partial(back_kernel, (nc, cr, col, tile)), out_s...]
    reduce_scatter x7 -> x0, waiting for transfers between devices: 486 us -> none  [the longest x5 312 us: scatter_rows(): return lax.psum_scatter(grad_full, 'fsdp', scatter_dimension=0, tiled=True)]
    dot_general x26 -> x0, matrix products: 435 us -> none  [the longest x21 394 us: matmul_f32(): return jnp.einsum(form, left, right, preferred_element_type=jnp.float32)]
    psum x1 -> x0, blocking collectives: 316 us -> none  [device_step(): lax.psum(jnp.concatenate([dk_part, dv_part], axis=-1).astype(jnp.float32)...]
    psum x1 -> x0, waiting for transfers between devices: 295 us -> none  [device_step(): branch_sum = lax.psum(branch_part, 'tp')]
    all_gather x7 -> x0, waiting for transfers between devices: 95.1 us -> none  [the longest x5 95.1 us: gather_rows(): return lax.all_gather(w_part, 'fsdp', axis=0, tiled=True)]
    convert_element_type x4 -> x0, other arithmetic: 24.6 us -> none  [the longest x1 21.7 us: device_step(): grad_x = (dy_out.astype(jnp.float32) + dx_norm).astype(jnp.bfloat16)]
    reduce_sum x3 -> x0, other arithmetic: 20.1 us -> none  [the longest x1 12.5 us: layer_norm(): return (x_cent * lax.rsqrt(x_var + 1e-05) * gain).astype(jnp.bfloat16)]
  transfers between devices with their start and end apart: 15 -> 0, of which waited for: 12 -> 0; matrix products, arithmetic and copies ran while one was open for 22% -> 0% of each run, Pallas kernels for 0% -> 0%
where the time goes in v1:
time: 814 us; the launch traced here: 812 us
  Pallas kernels  760 us (93%)
  local copies, waits for them, and re-layouts  37.7 us (5%)
  other arithmetic  13.1 us (2%)
    pallas_call x1, Pallas kernels, back_call(): pl.pallas_call(functools.partial(back_kernel, (nc, cr, col, tile)), out_s...  530 us
    pallas_call x1, Pallas kernels, front_call(): pl.pallas_call(functools.partial(front_kernel, (rt_rows, col)), out_shape...  215 us
    unnamed x22, local copies, waits for them, and re-layouts  30.1 us

profile of v1, /device:TPU:0, one launch (start us, length us, event | category | flops | bytes accessed | tf_op | source)
XLA Modules:
  0.0 811.9 jit_solution(16482086849395637434)
XLA Ops:
  0.7 1.3 broadcast_in_dim.2.gain
  1.9 1.7 pad_maximum_fusion.2.skv
  3.6 1.5 fusion.1
  5.1 0.9 pad_maximum_fusion.1.table
  6.0 2.4 pad_maximum_fusion.sod
  8.4 214.7 %forward.1 = (bf16[2048,4608]{1,0:T(8,128)(2,1)}, bf16[2048,512]{1,0:T(8,128)(2,1)}, bf16[2560,2048]{1,0:T(8,128)(2,1)}, f32[8,2048]{1,0:T(8,128)}, bf16[2304,20...) custom-call(bf16[2304,2048]{1,0:T(8,128)(2,1)} %bitcast.30, ...), custom_call_target="tpu_custom_call" | custom-call | flops 72477573120 | bytes 150000000 | tf_op jit(solution)/shard_map/forward/pallas_call | solution.py:358
  223.2 0.0 copy-start
  223.2 1.1 copy-done
  224.3 0.0 copy-start.1
  224.3 2.3 copy-done.1
  226.7 0.0 copy-start.5
  226.7 1.7 copy-done.5
  228.3 15.6 %attention.1 = (bf16[2304,512]{1,0:T(8,128)(2,1)S(1)}, bf16[2304,512]{1,0:T(8,128)(2,1)S(1)}, bf16[2304,512]{1,0:T(8,128)(2,1)S(1)}) custom-call(bf16[2304,1024]{1,0:T(8,128)(2,1)S(1)} %copy-done.1, bf16[2304,512]{1,0:T(8,128)(2,1)S(1)} %copy-done.5, f32[768,256]{1,0:T(8,128)S(1)} %copy-done), custom_call_target="tpu_custom_call" | custom-call | flops 12683575296 | bytes 20000000 | tf_op jit(solution)/shard_map/attention/pallas_call | solution.py:1174
  243.9 0.0 copy-start.2
  244.0 1.4 copy-done.2
  245.4 0.0 copy-start.3
  245.4 1.4 copy-done.3
  246.8 0.0 copy-start.4
  246.8 1.6 copy-done.4
  248.3 530.0 %backward.1 = (bf16[2304,2048]{1,0:T(8,128)(2,1)}, bf16[2304,2048]{1,0:T(8,128)(2,1)}, bf16[2,2304,2048]{2,1,0:T(8,128)(2,1)}, bf16[2,24,96,2048]{3,2,1,0:T(8,12...) custom-call(bf16[2304,512]{1,0:T(8,128)(2,1)} %copy-done.2, ...), custom_call_target="tpu_custom_call" | custom-call | flops 270582939648 | bytes 200000000 | tf_op jit(solution)/shard_map/backward/pallas_call | solution.py:1102
  778.3 0.0 copy-start.7
  778.3 1.4 slice_add_fusion
  779.7 1.3 add_bitcast_fusion
  781.0 0.8 fusion.3
  781.8 0.0 slice-start
  781.8 0.0 copy-done.7
  781.8 0.0 slice-start.1
  781.8 0.0 copy-start.6
  781.9 2.8 convert_add_fusion.3
  784.6 0.8 slice.79
  785.4 1.5 slice.82
  786.9 0.0 slice-done
  786.9 0.0 slice-done.1
  786.9 1.9 copy-done.6
  788.8 1.2 convert_add_fusion
  790.0 0.8 slice.76
  790.8 2.4 fusion.2
  793.2 9.4 %copy.22 = bf16[3,768,2048]{2,1,0:T(8,128)(2,1)} copy(bf16[3,768,2048]{2,1,0:T(8,128)(2,1)} %bitcast.26) | data formatting | bytes 18874368
  802.5 9.4 %copy.23 = bf16[3,768,2048]{2,1,0:T(8,128)(2,1)} copy(bf16[3,768,2048]{2,1,0:T(8,128)(2,1)} %bitcast.25) | data formatting | bytes 18874368
  (2 shorter events, 0.0 us)
Async XLA Ops:
  223.2 1.1 copy-start
  224.3 2.3 copy-start.1
  226.7 1.7 copy-start.5
  243.9 1.4 copy-start.2
  245.4 1.4 copy-start.3
  246.8 1.6 copy-start.4
  778.3 3.5 copy-start.7
  781.8 5.1 slice-start
  781.8 5.1 slice-start.1
  781.8 6.9 copy-start.6

commit v2 on v1

--- a/solution.py
+++ b/solution.py
@@ -33,13 +33,14 @@
     return lax.dot_general(left, right, ((dims[:1], dims[1:]), ((), ())), preferred_element_type=F32)
 
 
-def front_kernel(dims, x, dy, gain, sq, skv, sg, su, sod,
+def front_kernel(dims, x, dy, gain, sq, sk, sv, so, sd, sg, su,
                  wcat, wkv, wod, gain_all, h, qkv, gate, up, act, datt, dact,
-                 hv, wv, wodv, wqv, xt, yt, gt, et, b_q, b_kv, b_g, b_od, b_u, gv,
+                 hv, wv, wodv, wqv, xt, yt, gt, et, b_q, b_k, b_v, b_o, b_d, b_g, b_u, gv,
                  load, wload, keep, bsem, gsem, gain_s, gain_r, send, recv):
-    rt_rows, col = dims
+    rt_rows, split = dims
     tok, width = x.shape
-    inner, kv, ff = sq.shape[ONE], skv.shape[ONE], sg.shape[ONE]
+    inner, head, ff = sq.shape[ONE], sk.shape[ONE], sg.shape[ONE]
+    kv = TWO * head
     blk = sq.shape[ZERO]
     ka = inner + ff
     n = tok // rt_rows
@@ -53,17 +54,19 @@
                                             device_id_type=pl.DeviceIdType.MESH)
 
     items = (
-        (sq, wcat, TWO * ff, inner), (skv, wkv, ZERO, kv), (sg, wcat, ZERO, ff), (sod, wod, ZERO, blk), (su, wcat, ff, ff),
+        (sq, wcat, TWO * ff, inner, False), (sk, wkv, ZERO, head, False), (sv, wkv, head, head, False),
+        (so, wod, ZERO, inner, True), (sd, wod, inner, ff, True), (sg, wcat, ZERO, ff, False), (su, wcat, ff, ff, False),
     )
+    group_q, group_o, group_g, group_u = (ZERO, ONE, TWO), (THREE, 4), (5,), (6,)
 
     def block(i, mask, part=None):
-        _, full, at, wide = items[i]
+        _, whole_w, at, wide, tall = items[i]
         at_blk = pl.multiple_of((me ^ mask) * blk, blk)
-        if i == THREE:
-            rows = pl.ds(ZERO, ka) if part is None else pl.ds(part * (ka // TWO), ka // TWO)
-            return full.at[rows, pl.ds(at_blk, blk)]
+        if tall:
+            rows = pl.ds(at, wide) if part is None else pl.ds(at + part * (wide // TWO), wide // TWO)
+            return whole_w.at[rows, pl.ds(at_blk, blk)]
         rows = pl.ds(at_blk, blk) if part is None else pl.ds(at_blk + part * (blk // TWO), blk // TWO)
-        return full.at[rows, pl.ds(at, wide)]
+        return whole_w.at[rows, pl.ds(at, wide)]
 
     def own_to(i, to, num):
         return remote(items[i][ZERO], block(i, ZERO), send.at[i, num], recv.at[i, num], to)
@@ -74,31 +77,35 @@
     def arrived(i, mask, to, num, part=None):
         remote(block(i, mask, part), block(i, mask, part), send.at[i, num], recv.at[i, num], to).wait_recv()
 
-    def depart(i):
-        own_to(i, TWO, ZERO).start()
-        own_to(i, 4, ONE).start()
-        own_to(i, ONE, 4).start()
-
-    def relay(i):
-        arrived(i, TWO, TWO, ZERO)
-        pass_to(i, TWO, 4, TWO, ZERO).start()
-        arrived(i, 4, 4, ONE)
-        pass_to(i, 4, TWO, THREE, ONE).start()
-        pass_to(i, TWO, ONE, 5).start()
-        pass_to(i, 4, ONE, 6).start()
-
-    def corner(i):
-        arrived(i, 6, 4, TWO, ZERO)
-        pass_to(i, 6, ONE, 7, ZERO).start()
-        arrived(i, 6, TWO, THREE, ONE)
-        pass_to(i, 6, ONE, 8, ONE).start()
-
-    def full(i):
-        arrived(i, ONE, ONE, 4)
-        arrived(i, THREE, ONE, 5)
-        arrived(i, 5, ONE, 6)
-        arrived(i, 7, ONE, 7, ZERO)
-        arrived(i, 7, ONE, 8, ONE)
+    def depart(group):
+        for i in group:
+            own_to(i, TWO, ZERO).start()
+            own_to(i, 4, ONE).start()
+            own_to(i, ONE, 4).start()
+
+    def relay(group):
+        for i in group:
+            arrived(i, TWO, TWO, ZERO)
+            pass_to(i, TWO, 4, TWO, ZERO).start()
+            arrived(i, 4, 4, ONE)
+            pass_to(i, 4, TWO, THREE, ONE).start()
+            pass_to(i, TWO, ONE, 5).start()
+            pass_to(i, 4, ONE, 6).start()
+
+    def corner(group):
+        for i in group:
+            arrived(i, 6, 4, TWO, ZERO)
+            pass_to(i, 6, ONE, 7, ZERO).start()
+            arrived(i, 6, TWO, THREE, ONE)
+            pass_to(i, 6, ONE, 8, ONE).start()
+
+    def full(group):
+        for i in group:
+            arrived(i, ONE, ONE, 4)
+            arrived(i, THREE, ONE, 5)
+            arrived(i, 5, ONE, 6)
+            arrived(i, 7, ONE, 7, ZERO)
+            arrived(i, 7, ONE, 8, ONE)
 
     def sent(i):
         own_to(i, TWO, ZERO).wait_send()
@@ -111,7 +118,7 @@
         pass_to(i, 6, ONE, 7, ZERO).wait_send()
         pass_to(i, 6, ONE, 8, ONE).wait_send()
 
-    bounce = (b_q, b_kv, b_g, b_od, b_u)
+    bounce = (b_q, b_k, b_v, b_o, b_d, b_g, b_u)
 
     def own_in(i):
         return local(items[i][ZERO], bounce[i], bsem.at[i])
@@ -129,14 +136,16 @@
 
         lax.fori_loop(ZERO, n, body, ZERO)
 
-    def dot_cols(left, weight, dims_, out, wide, at=ZERO):
+    def dot_cols(left, weight, dims_, out, wide):
+        col = wide // split
+
         def body(j, carry):
             cs = pl.ds(pl.multiple_of(j * col, col), col)
             rhs = weight[:, cs] if dims_[ONE] == ZERO else weight[cs, :]
-            out[:, pl.ds(pl.multiple_of(at + j * col, col), col)] = contract(left[...], rhs, dims_).astype(BF16)
+            out[:, cs] = contract(left[...], rhs, dims_).astype(BF16)
             return carry
 
-        lax.fori_loop(ZERO, wide // col, body, ZERO)
+        lax.fori_loop(ZERO, split, body, ZERO)
 
     def gain_cols(mask):
         return pl.ds(pl.multiple_of((me ^ mask) * blk, blk), blk)
@@ -153,15 +162,15 @@
     peers = range(ONE, 8)
     for m in peers:
         gain_to(m).start()
-    for i in range(THREE):
-        depart(i)
+    depart(group_q)
     gain_in(ZERO).start()
-    for i in range(5):
+    n_items = len(items)
+    for i in range(n_items):
         own_in(i).start()
     for m in peers:
         gain_from(m).wait_recv()
         gain_in(m).start()
-    for i in range(5):
+    for i in range(n_items):
         own_in(i).wait()
         own_out(i).start()
     for m in range(8):
@@ -196,19 +205,19 @@
 
         h_keep(k).start()
 
+        @pl.when(k == n // TWO)
+        def _():
+            relay(group_q)
+            depart(group_o)
+
     tiles(norm)
     h_keep(n - TWO).wait()
     h_keep(n - ONE).wait()
 
-    for i in range(THREE):
-        relay(i)
-    depart(THREE)
-    for i in range(TWO):
-        corner(i)
-    for i in range(5):
+    corner(group_q)
+    for i in range(n_items):
         own_out(i).wait()
-    for i in range(TWO):
-        full(i)
+    full(group_q)
     w0 = local(wcat.at[:, pl.ds(TWO * ff, inner)], wqv.at[:, pl.ds(ZERO, inner)], wload.at[ZERO])
     w1 = local(wkv, wqv.at[:, pl.ds(inner, kv)], wload.at[ONE])
     w0.start()
@@ -216,102 +225,112 @@
     w0.wait()
     w1.wait()
 
-    def out_keep(k, src, dst, which):
-        return local(src, dst.at[tile_rows(k)], keep.at[which])
+    def after_store(k, copies):
+        @pl.when(k >= TWO)
+        def _():
+            for c in copies(k - TWO):
+                c.wait()
+
+    def stored(copies):
+        for k in range(max(n - TWO, ZERO), n):
+            for c in copies(k):
+                c.wait()
+
+    def half(ref, k, at, wide):
+        return ref.at[lax.rem(k, TWO), :, pl.ds(at, wide)]
+
+    def qkv_keep(k):
+        return (local(half(yt, k, ZERO, inner + kv), qkv.at[tile_rows(k)], keep.at[lax.rem(k, TWO)]),)
 
     def qkv_tile(k):
-        @pl.when(k >= ONE)
-        def _():
-            out_keep(k - ONE, yt.at[:, pl.ds(ZERO, inner + kv)], qkv, TWO).wait()
-
-        dot_cols(hv.at[tile_rows(k)], wqv, (ONE, ZERO), yt, inner + kv)
-        out_keep(k, yt.at[:, pl.ds(ZERO, inner + kv)], qkv, TWO).start()
+        after_store(k, qkv_keep)
+        dot_cols(hv.at[tile_rows(k)], wqv, (ONE, ZERO), yt.at[lax.rem(k, TWO)], inner + kv)
+        for c in qkv_keep(k):
+            c.start()
 
     tiles(qkv_tile)
-    out_keep(n - ONE, yt.at[:, pl.ds(ZERO, inner + kv)], qkv, TWO).wait()
-
-    corner(TWO)
-    full(TWO)
-    w2 = local(wcat.at[:, pl.ds(ZERO, ff)], wv, wload.at[TWO])
+    stored(qkv_keep)
+
+    def dy_load(k):
+        return local(dy.at[tile_rows(k)], xt.at[lax.rem(k, TWO)], load.at[lax.rem(k, TWO)])
+
+    dy_load(ZERO).start()
+    relay(group_o)
+    depart(group_g)
+    corner(group_o)
+    full(group_o)
+    w2 = local(wod, wodv, wload.at[TWO])
     w2.start()
     w2.wait()
 
-    def gate_tile(k):
-        @pl.when(k >= ONE)
-        def _():
-            out_keep(k - ONE, yt.at[:, pl.ds(ZERO, ff)], gate, TWO).wait()
-
-        dot_cols(hv.at[tile_rows(k)], wv, (ONE, ZERO), yt, ff)
-        out_keep(k, yt.at[:, pl.ds(ZERO, ff)], gate, TWO).start()
-
-    tiles(gate_tile)
-    out_keep(n - ONE, yt.at[:, pl.ds(ZERO, ff)], gate, TWO).wait()
-
-    def dy_load(k):
-        return local(dy.at[tile_rows(k)], xt.at[lax.rem(k, TWO)], load.at[lax.rem(k, TWO)])
-
-    dy_load(ZERO).start()
-    relay(THREE)
-    depart(4)
-    corner(THREE)
-    full(THREE)
-    w3 = local(wod, wodv, wload.at[THREE])
+    def back_keep(k):
+        return (local(half(yt, k, ZERO, inner), datt.at[tile_rows(k)], keep.at[lax.rem(k, TWO)]),
+                local(half(yt, k, inner, ff), dact.at[tile_rows(k)], keep.at[TWO + lax.rem(k, TWO)]))
+
+    def back_tile(k):
+        dy_load(k).wait()
+
+        @pl.when(k + ONE < n)
+        def _():
+            dy_load(k + ONE).start()
+
+        after_store(k, back_keep)
+        dot_cols(xt.at[lax.rem(k, TWO)], wodv, (ONE, ONE), yt.at[lax.rem(k, TWO)], ka)
+        for c in back_keep(k):
+            c.start()
+
+        @pl.when(k == n // TWO)
+        def _():
+            relay(group_g)
+            depart(group_u)
+
+    tiles(back_tile)
+    stored(back_keep)
+
+    corner(group_g)
+    full(group_g)
+    w3 = local(wcat.at[:, pl.ds(ZERO, ff)], wv, wload.at[THREE])
     w3.start()
     w3.wait()
 
-    def back_keeps(k):
-        return (local(yt.at[:, pl.ds(ZERO, inner)], datt.at[tile_rows(k)], keep.at[TWO]),
-                local(yt.at[:, pl.ds(inner, ff)], dact.at[tile_rows(k)], keep.at[THREE]))
-
-    def back_tile(k):
-        dy_load(k).wait()
-
-        @pl.when(k + ONE < n)
-        def _():
-            dy_load(k + ONE).start()
-
-        @pl.when(k == (TWO * n) // THREE)
-        def _():
-            relay(4)
-
-        @pl.when(k >= ONE)
-        def _():
-            for c in back_keeps(k - ONE):
-                c.wait()
-
-        dot_cols(xt.at[lax.rem(k, TWO)], wodv, (ONE, ONE), yt, ka)
-        for c in back_keeps(k):
+    def gate_keep(k):
+        return (local(half(yt, k, ZERO, ff), gate.at[tile_rows(k)], keep.at[lax.rem(k, TWO)]),)
+
+    def gate_tile(k):
+        after_store(k, gate_keep)
+        dot_cols(hv.at[tile_rows(k)], wv, (ONE, ZERO), yt.at[lax.rem(k, TWO)], ff)
+        for c in gate_keep(k):
             c.start()
 
-    tiles(back_tile)
-    for c in back_keeps(n - ONE):
-        c.wait()
+        @pl.when(k == n // TWO)
+        def _():
+            relay(group_u)
+
+    tiles(gate_tile)
+    stored(gate_keep)
 
     def gate_load(k):
         return local(gate.at[tile_rows(k)], gt, load.at[TWO])
 
     gate_load(ZERO).start()
-    corner(4)
-    full(4)
+    corner(group_u)
+    full(group_u)
     w4 = local(wcat.at[:, pl.ds(ff, ff)], wv, wload.at[4])
     w4.start()
     w4.wait()
 
-    def up_keeps(k):
-        return (local(yt.at[:, pl.ds(ZERO, ff)], up.at[tile_rows(k)], keep.at[TWO]), local(et, act.at[tile_rows(k)], keep.at[THREE]))
+    def up_keep(k):
+        return (local(half(yt, k, ZERO, ff), up.at[tile_rows(k)], keep.at[lax.rem(k, TWO)]),
+                local(et.at[lax.rem(k, TWO)], act.at[tile_rows(k)], keep.at[TWO + lax.rem(k, TWO)]))
 
     def up_tile(k):
-        @pl.when(k >= ONE)
-        def _():
-            for c in up_keeps(k - ONE):
-                c.wait()
-
-        dot_cols(hv.at[tile_rows(k)], wv, (ONE, ZERO), yt, ff)
+        after_store(k, up_keep)
+        dot_cols(hv.at[tile_rows(k)], wv, (ONE, ZERO), yt.at[lax.rem(k, TWO)], ff)
         gate_load(k).wait()
 
         def rows(sl):
             g = gt[sl, :].astype(F32)
-            et[sl, :] = (g * jax.nn.sigmoid(g) * yt[sl, ZERO:ff].astype(F32)).astype(BF16)
+            et[lax.rem(k, TWO), sl, :] = (g * jax.nn.sigmoid(g) * yt[lax.rem(k, TWO), sl, ZERO:ff].astype(F32)).astype(BF16)
 
         row_loop(rt_rows, rows)
 
@@ -319,13 +338,12 @@
         def _():
             gate_load(k + ONE).start()
 
-        for c in up_keeps(k):
+        for c in up_keep(k):
             c.start()
 
     tiles(up_tile)
-    for c in up_keeps(n - ONE):
-        c.wait()
-    for i in range(5):
+    stored(up_keep)
+    for i in range(n_items):
         sent(i)
     for m in peers:
         gain_to(m).wait_send()
@@ -334,11 +352,13 @@
     g_out.wait()
 
 
-def front_call(x, dy, gain, sq, skv, sg, su, sod, rt_rows=384, col=512):
+def front_call(x, dy, gain, shards, rt_rows=384, split=2):
+    sq, sk, sv, so, sd, sg, su = shards
     tok, width = x.shape
-    inner, kv, ff = sq.shape[1], skv.shape[1], sg.shape[1]
+    inner, ff = sq.shape[1], sg.shape[1]
+    kv = 2 * sk.shape[1]
+    ka = inner + ff
     blk = sq.shape[0]
-    ka = inner + ff
     shape = jax.ShapeDtypeStruct
     outs = (
         shape((width, 2 * ff + inner), BF16), shape((width, kv), BF16), shape((ka, width), BF16), shape((8, width), F32),
@@ -348,23 +368,23 @@
     sems = pltpu.SemaphoreType.DMA
     scratch = [
         pltpu.VMEM((tok, width), BF16), pltpu.VMEM((width, ff), BF16), pltpu.VMEM((ka, width), BF16), pltpu.VMEM((width, inner + kv), BF16),
-        pltpu.VMEM((2, rt_rows, width), BF16), pltpu.VMEM((rt_rows, max(ka, inner + kv)), BF16), pltpu.VMEM((rt_rows, ff), BF16),
-        pltpu.VMEM((rt_rows, ff), BF16), pltpu.VMEM(sq.shape, BF16), pltpu.VMEM(skv.shape, BF16), pltpu.VMEM(sg.shape, BF16), pltpu.VMEM(sod.shape, BF16), pltpu.VMEM(su.shape, BF16),
+        pltpu.VMEM((2, rt_rows, width), BF16), pltpu.VMEM((2, rt_rows, max(ka, inner + kv)), BF16), pltpu.VMEM((rt_rows, ff), BF16),
+        pltpu.VMEM((2, rt_rows, ff), BF16), *[pltpu.VMEM(w.shape, BF16) for w in shards],
         pltpu.VMEM((8, width), F32),
-        sems((3,)), sems((5,)), sems((4,)), sems((5,)), sems((8,)), sems((7,)), sems((7,)), sems((5, 9)), sems((5, 9)),
+        sems((3,)), sems((5,)), sems((4,)), sems((7,)), sems((8,)), sems((7,)), sems((7,)), sems((7, 9)), sems((7, 9)),
     ]
     flops = 2 * tok * width * (2 * ka + ff + kv)
     anywhere = pl.BlockSpec(memory_space=pl.ANY)
     return pl.pallas_call(
-        functools.partial(front_kernel, (rt_rows, col)),
+        functools.partial(front_kernel, (rt_rows, split)),
         out_shape=outs,
-        in_specs=[anywhere] * 8,
+        in_specs=[anywhere] * 10,
         out_specs=tuple(anywhere for _ in outs),
         scratch_shapes=scratch,
         cost_estimate=pl.CostEstimate(flops=flops, bytes_accessed=150_000_000, transcendentals=tok * ff),
         compiler_params=pltpu.CompilerParams(vmem_limit_bytes=67_000_000, has_side_effects=True),
         name='forward',
-    )(x, dy, gain, sq, skv, sg, su, sod)
+    )(x, dy, gain, *shards)
 
 
 def back_kernel(dims, att, act, wod, gate, up, dact, dq, wcat, wkv, dkv, table, h, dy, x, gain,
@@ -975,7 +995,6 @@
                 kv_send(i).wait_send()
 
     out_weights().start()
-    in_weights().start()
     gv[8:16, :] = jnp.zeros((8, width), F32)
     small = [local(gain, gv.at[pl.ds(ZERO, 8)], load.at[ZERO]), local(wkv, wv, load.at[ONE]), local(table, tv, load.at[TWO])]
     for s in small:
@@ -1008,6 +1027,7 @@
             @pl.when(s == ZERO)
             def _():
                 out_weights().wait()
+                in_weights().start()
 
             y_step(s)
 
@@ -1064,7 +1084,7 @@
     kv_settle()
 
 
-def back_call(att, act, wod, gate, up, dact, dq, wcat, wkv, dkv, table, h, dy, x, gain, nc=12, col=512, tile=512):
+def back_call(att, act, wod, gate, up, dact, dq, wcat, wkv, dkv, table, h, dy, x, gain, nc=12, col=1024, tile=512):
     tok, width = h.shape
     inner, ff = att.shape[1], act.shape[1]
     ka, kb, kv = inner + ff, wcat.shape[1], dkv.shape[1]
@@ -1179,9 +1199,57 @@
         out_specs=(rows(inner), rows(inner), rows(2 * head)),
         scratch_shapes=[pltpu.VMEM((n_pos, head), BF16), pltpu.VMEM((n_pos, head), F32), pltpu.VMEM((n_pos, head), F32)],
         cost_estimate=pl.CostEstimate(flops=flops, bytes_accessed=20_000_000, transcendentals=n_batch * heads * n_pos * n_pos),
-        compiler_params=pltpu.CompilerParams(vmem_limit_bytes=40_000_000),
+        compiler_params=pltpu.CompilerParams(vmem_limit_bytes=67_000_000),
         name='attention',
     )(qkv, datt, table)
+
+
+def finish_kernel(y, gx, own_o, own_d, got_o, got_d, own_b, got_b, kvs, y_out, gx_out, o_out, d_out, g_out, u_out, q_out, k_out, v_out):
+    y_out[...] = y[...]
+    gx_out[...] = gx[...]
+
+    def total(own, got):
+        return own[...] + got[0].astype(F32) + got[1].astype(F32) + got[2].astype(F32)
+
+    o_out[...] = total(own_o, got_o)
+    d_out[...] = total(own_d, got_d)
+    ff, inner, head = g_out.shape[1], q_out.shape[1], k_out.shape[1]
+    at = 0
+    for out in (g_out, u_out, q_out):
+        cols = slice(at, at + out.shape[1])
+        out[...] = own_b[:, cols] + got_b[0, :, cols].astype(F32) + got_b[1, :, cols].astype(F32) + got_b[2, :, cols].astype(F32)
+        at += out.shape[1]
+    k_out[...] = kvs[0, :, 0:head] + kvs[1, :, 0:head]
+    v_out[...] = kvs[0, :, head:] + kvs[1, :, head:]
+
+
+def finish_call(y, gx, own_a, got_a, own_b, got_b, kvs, inner, ff, steps=16):
+    tok, width = y.shape
+    blk, wide = own_b.shape
+    kv = kvs.shape[2]
+    skip = inner // (ff // steps)
+    shape = jax.ShapeDtypeStruct
+
+    def rows(n, cols, off=0):
+        return pl.BlockSpec((n // steps, cols), lambda i: (i + off, 0))
+
+    def three(n, cols, off=0):
+        return pl.BlockSpec((3, n // steps, cols), lambda i: (0, i + off, 0))
+
+    used = 2 * ff + inner
+    return pl.pallas_call(
+        finish_kernel,
+        grid=(steps,),
+        out_shape=(shape((tok, width), BF16), shape((tok, width), BF16), shape((inner, blk), F32), shape((ff, blk), F32),
+                   shape((blk, ff), F32), shape((blk, ff), F32), shape((blk, inner), F32), shape((blk, kv // 2), F32), shape((blk, kv // 2), F32)),
+        in_specs=[rows(tok, width), rows(tok, width), rows(inner, blk), rows(ff, blk, skip), three(inner, blk), three(ff, blk, skip),
+                  rows(blk, used), three(blk, used), pl.BlockSpec((2, blk // steps, kv), lambda i: (0, i, 0))],
+        out_specs=(rows(tok, width), rows(tok, width), rows(inner, blk), rows(ff, blk), rows(blk, ff), rows(blk, ff), rows(blk, inner),
+                   rows(blk, kv // 2), rows(blk, kv // 2)),
+        cost_estimate=pl.CostEstimate(flops=8 * blk * wide, bytes_accessed=66_000_000, transcendentals=0),
+        compiler_params=pltpu.CompilerParams(vmem_limit_bytes=67_000_000),
+        name='finish',
+    )(y, gx, own_a, own_a, got_a, got_a, own_b, got_b, kvs)
 
 
 def solution(mesh):
@@ -1196,23 +1264,16 @@
         table = jnp.concatenate(rope_tables(seq_len, head_dim), axis=-1)
 
         gain8 = jnp.broadcast_to(ln_gain[None, :], (8, ln_gain.shape[0]))
-        front = front_call(x_rows, dy, gain8, w_q, jnp.concatenate([w_k, w_v], axis=1), w_gate, w_up, jnp.concatenate([w_o, w_down], axis=0))
+        front = front_call(x_rows, dy, gain8, (w_q, w_k, w_v, w_o, w_down, w_gate, w_up))
         wcat, wkv, wod, gain, h_norm, qkv, gate, up, act, d_att, d_act = front
         att, d_q, dkv = attention_call(qkv, d_att, table, n_batch)
         res = back_call(att, act, wod, gate, up, d_act, d_q, wcat, wkv, dkv, table, h_norm, dy, x_rows, gain)
-        y_rows, gx_rows = res[0], res[1]
         own_a, own_b, got_a, got_b, gsum, _, kvsum = res[9:16]
-
-        def total(own, got):
-            return own + got[0].astype(F32) + got[1].astype(F32) + got[2].astype(F32)
-
-        grad_od = total(own_a, got_a)
-        big = 2 * ff + inner
-        grad_in = total(own_b[:, :big], got_b[:, :, :big])
-        grad_kv = kvsum[0] + kvsum[1]
+        done = finish_call(res[0], res[1], own_a, got_a, own_b, got_b, kvsum, inner, ff)
+        y_rows, gx_rows, grad_wo, grad_wdown, grad_wgate, grad_wup, grad_wq, grad_wk, grad_wv = done
         grad_gain = gsum[0, 0] + gsum[1, 0]
-        return (y_rows.reshape(x_in.shape), gx_rows.reshape(x_in.shape), grad_gain, grad_in[:, 2 * ff:2 * ff + inner],
-                grad_kv[:, :head_dim], grad_kv[:, head_dim:], grad_od[:inner], grad_in[:, :ff], grad_in[:, ff:2 * ff], grad_od[inner:])
+        return (y_rows.reshape(x_in.shape), gx_rows.reshape(x_in.shape), grad_gain, grad_wq, grad_wk, grad_wv,
+                grad_wo, grad_wgate, grad_wup, grad_wdown)
 
     act_spec = P('fsdp', None, None)
     row_spec = P('fsdp', 'tp')

time: 814 us -> 765 us (0.940)
  local copies, waits for them, and re-layouts: 37.7 us -> 1.28 us
  other arithmetic: 13.1 us -> 3.68 us
    unnamed x22 -> x0, local copies, waits for them, and re-layouts: 30.1 us -> none
    pallas_call x1 -> x2, Pallas kernels: 215 us -> 208 us  [the longest x1 183 us: front_call(): pl.pallas_call(functools.partial(front_kernel, (rt_rows, split)), out_sha...]
where the time goes in v2:
time: 765 us; the launch traced here: 763 us
  Pallas kernels  757 us (99%)
    pallas_call x1, Pallas kernels, back_call(): pl.pallas_call(functools.partial(back_kernel, (nc, cr, col, tile)), out_s...  530 us
    pallas_call x1, Pallas kernels, front_call(): pl.pallas_call(functools.partial(front_kernel, (rt_rows, split)), out_sha...  183 us
    pallas_call x1, Pallas kernels, finish_call(): pl.pallas_call(finish_kernel, grid=(steps,), out_shape=(shape((tok, width...  25 us
    pallas_call x1, Pallas kernels, attention_call(): pl.pallas_call(functools.partial(attention_kernel, heads), grid=(n_batch,...  18.9 us

profile of v2, /device:TPU:0, one launch (start us, length us, event | category | flops | bytes accessed | tf_op | source)
XLA Modules:
  0.0 762.8 jit_solution(14730489811185287250)
XLA Ops:
  0.7 1.3 broadcast_in_dim.2.gain
  1.9 1.5 fusion.1
  3.4 0.9 pad_maximum_fusion.table
  4.3 183.5 %forward.1 = (bf16[2048,4608]{1,0:T(8,128)(2,1)}, bf16[2048,512]{1,0:T(8,128)(2,1)}, bf16[2560,2048]{1,0:T(8,128)(2,1)}, f32[8,2048]{1,0:T(8,128)}, bf16[2304,20...) custom-call(bf16[2304,2048]{1,0:T(8,128)(2,1)} %bitcast.6, ...), custom_call_target="tpu_custom_call" | custom-call | flops 72477573120 | bytes 150000000 | tf_op jit(solution)/shard_map/forward/pallas_call | solution.py:378
  187.8 18.9 %attention.1 = (bf16[2304,512]{1,0:T(8,128)(2,1)}, bf16[2304,512]{1,0:T(8,128)(2,1)}, bf16[2304,512]{1,0:T(8,128)(2,1)}) custom-call(bf16[2304,1024]{1,0:T(8,128)(2,1)} %get-tuple-element.41.qkv, bf16[2304,512]{1,0:T(8,128)(2,1)} %get-tuple-element.42.datt, f32[768,256]{1,0:T(8,128)} %pad_maximum_fusion.table), custom_call_target="tpu_custom_call" | custom-call | flops 12683575296 | bytes 20000000 | tf_op jit(solution)/shard_map/attention/pallas_call | solution.py:1194
  206.8 529.8 %backward.1 = (bf16[2304,2048]{1,0:T(8,128)(2,1)}, bf16[2304,2048]{1,0:T(8,128)(2,1)}, bf16[2,2304,2048]{2,1,0:T(8,128)(2,1)}, bf16[2,24,96,2048]{3,2,1,0:T(8,12...) custom-call(bf16[2304,512]{1,0:T(8,128)(2,1)} %get-tuple-element.43., ...), custom_call_target="tpu_custom_call" | custom-call | flops 270582939648 | bytes 200000000 | tf_op jit(solution)/shard_map/backward/pallas_call | solution.py:1122
  736.6 25.0 %finish.1 = (bf16[2304,2048]{1,0:T(8,128)(2,1)}, bf16[2304,2048]{1,0:T(8,128)(2,1)}, f32[512,256]{1,0:T(8,128)}, f32[2048,256]{1,0:T(8,128)}, f32[256,2048]{1,0:...) custom-call(bf16[2304,2048]{1,0:T(8,128)(2,1)} %get-tuple-element.55.y, ...), custom_call_target="tpu_custom_call" | custom-call | flops 10485760 | bytes 66000000 | tf_op jit(solution)/shard_map/finish/pallas_call | solution.py:1240
  761.5 1.3 slice_add_fusion
  (1 shorter events, 0.0 us)

commit v3 on v2

--- a/solution.py
+++ b/solution.py
@@ -404,8 +404,8 @@
     na, nb = ka // tile, (kb + kv) // tile
     depth = THREE
     last = THREE
-    hop_lag = TWO
-    end = TWO * nc - ONE + hop_lag * (last + TWO)
+    hop_lag, pass_lag = ONE, ONE
+    end = TWO * nc - ONE + hop_lag * last + pass_lag * TWO
     me = lax.axis_index('fsdp')
     z = lax.axis_index('tp')
 
@@ -610,7 +610,7 @@
                         keep_kv.wait()
                         keep_h.wait()
 
-            e = t - hop_lag * (last + ONE) - hop_lag * (TWO - rank)
+            e = t - hop_lag * last - pass_lag * (last - rank)
 
             def pass_on():
                 @pl.when(((rank == ONE) | (rank == TWO)) & (e >= ZERO) & (e < TWO * nc))
@@ -1072,7 +1072,7 @@
         def _():
             kv_total()
 
-        @pl.when(s == end - hop_lag * TWO + ONE)
+        @pl.when(s == TWO * nc + hop_lag * last)
         def _():
             gain_total()
 

time: 765 us -> 750 us (0.980)
  Pallas kernels: 757 us -> 742 us
    pallas_call x1, Pallas kernels: 530 us -> 514 us  [back_call(): pl.pallas_call(functools.partial(back_kernel, (nc, cr, col, tile)), out_s...]
where the time goes in v3:
time: 750 us; the launch traced here: 747 us
  Pallas kernels  742 us (99%)
    pallas_call x1, Pallas kernels, back_call(): pl.pallas_call(functools.partial(back_kernel, (nc, cr, col, tile)), out_s...  514 us
    pallas_call x1, Pallas kernels, front_call(): pl.pallas_call(functools.partial(front_kernel, (rt_rows, split)), out_sha...  183 us
    pallas_call x1, Pallas kernels, finish_call(): pl.pallas_call(finish_kernel, grid=(steps,), out_shape=(shape((tok, width...  25 us
    pallas_call x1, Pallas kernels, attention_call(): pl.pallas_call(functools.partial(attention_kernel, heads), grid=(n_batch,...  18.9 us

profile of v3, /device:TPU:0, one launch (start us, length us, event | category | flops | bytes accessed | tf_op | source)
XLA Modules:
  0.0 747.4 jit_solution(9153689539340132138)
XLA Ops:
  0.7 1.3 broadcast_in_dim.2.gain
  1.9 1.5 fusion.1
  3.4 0.9 pad_maximum_fusion.table
  4.3 183.5 %forward.1 = (bf16[2048,4608]{1,0:T(8,128)(2,1)}, bf16[2048,512]{1,0:T(8,128)(2,1)}, bf16[2560,2048]{1,0:T(8,128)(2,1)}, f32[8,2048]{1,0:T(8,128)}, bf16[2304,20...) custom-call(bf16[2304,2048]{1,0:T(8,128)(2,1)} %bitcast.6, ...), custom_call_target="tpu_custom_call" | custom-call | flops 72477573120 | bytes 150000000 | tf_op jit(solution)/shard_map/forward/pallas_call | solution.py:378
  187.8 18.9 %attention.1 = (bf16[2304,512]{1,0:T(8,128)(2,1)}, bf16[2304,512]{1,0:T(8,128)(2,1)}, bf16[2304,512]{1,0:T(8,128)(2,1)}) custom-call(bf16[2304,1024]{1,0:T(8,128)(2,1)} %get-tuple-element.41.qkv, bf16[2304,512]{1,0:T(8,128)(2,1)} %get-tuple-element.42.datt, f32[768,256]{1,0:T(8,128)} %pad_maximum_fusion.table), custom_call_target="tpu_custom_call" | custom-call | flops 12683575296 | bytes 20000000 | tf_op jit(solution)/shard_map/attention/pallas_call | solution.py:1194
  206.8 514.4 %backward.1 = (bf16[2304,2048]{1,0:T(8,128)(2,1)}, bf16[2304,2048]{1,0:T(8,128)(2,1)}, bf16[2,2304,2048]{2,1,0:T(8,128)(2,1)}, bf16[2,24,96,2048]{3,2,1,0:T(8,12...) custom-call(bf16[2304,512]{1,0:T(8,128)(2,1)} %get-tuple-element.43., ...), custom_call_target="tpu_custom_call" | custom-call | flops 270582939648 | bytes 200000000 | tf_op jit(solution)/shard_map/backward/pallas_call | solution.py:1122
  721.2 25.0 %finish.1 = (bf16[2304,2048]{1,0:T(8,128)(2,1)}, bf16[2304,2048]{1,0:T(8,128)(2,1)}, f32[512,256]{1,0:T(8,128)}, f32[2048,256]{1,0:T(8,128)}, f32[256,2048]{1,0:...) custom-call(bf16[2304,2048]{1,0:T(8,128)(2,1)} %get-tuple-element.55.y, ...), custom_call_target="tpu_custom_call" | custom-call | flops 10485760 | bytes 66000000 | tf_op jit(solution)/shard_map/finish/pallas_call | solution.py:1240
  746.1 1.3 slice_add_fusion
  (1 shorter events, 0.0 us)
